TPU v7x, 32 devices: a whole 2x2x4 slice. The times are simulated.
32 devices in a mesh: dp: 2 (over x), tp: 16 (over y, z, core).
Axes of the slice: x: 2, y: 2, z: 4, core: 2. Of those that a mesh axis runs over, the one named last changes fastest.
Arguments:
- x: bfloat16 [8192, 4096], P(('dp', 'tp')), parts along dimension 0
- dy: bfloat16 [8192, 4096], P(('dp', 'tp')), parts along dimension 0
- pre: bfloat16 [8192, 16384], P('dp', 'tp'), parts along dimension 0
- w_in: bfloat16 [4096, 16384], P(None, 'tp')
- w_down: bfloat16 [16384, 4096], P('tp')
Outputs:
- output 1: bfloat16 [8192, 4096], P(('dp', 'tp')), parts along dimension 0
- output 2: bfloat16 [8192, 16384], P('dp', 'tp'), parts along dimension 0
- output 3: bfloat16 [32768, 4096], P(('dp', 'tp')), parts along dimension 0
There are 2 independent parts. A program takes and returns all parts, laid end to end along the dimension named above; an argument that names none is the same for every part.
All inputs are finite; a program needn't handle non-finite values.
Results may differ from a plain program's by a relative error of at most 0.012.
Values are sent between devices in bfloat16 or wider.
A program may use at most 2 GiB of HBM per device.

v0:
```python
import jax
import jax.numpy as jnp


def act(pre):
    return jnp.square(jax.nn.relu(pre))


def solution(mesh):
    def step(x, dy, pre, w_in, w_down):
        hidden, back = jax.vjp(act, pre.astype(jnp.float32))
        d_hidden = jnp.dot(dy, w_down.T, preferred_element_type=jnp.float32)
        d_pre = back(d_hidden)[0].astype(jnp.bfloat16)
        dx = jnp.dot(d_pre, w_in.T)
        groups = mesh.shape["dp"]

        def by_group(a, b):
            a, b = (t.reshape(groups, -1, t.shape[-1]) for t in (a, b))
            product = jnp.einsum("gta,gtb->gab", a, b, preferred_element_type=jnp.float32)
            return product.astype(jnp.bfloat16).reshape(-1, b.shape[-1])

        return dx, by_group(x, d_pre), by_group(hidden.astype(jnp.bfloat16), dy)

    return step
```

profile of v0, /device:TPU:0, one launch (start us, length us, event | category | flops | bytes accessed | tf_op | source)
XLA Modules:
  0.0 1348.9 jit_solution(15477746053169048119)
XLA Ops:
  13.6 170.8 %all-gather.5.cloned.1.call-done = bf16[4096,4096]{1,0:T(8,128)(2,1)} async-done(((bf16[256,4096]{1,0:T(8,128)(2,1)}), bf16[4096,4096]{1,0:T(8,128)(2,1)}) %all-gather.5.cloned.1.call-update) | async-done | bytes 33554448 | tf_op args[1]
  184.4 43.9 %fusion.34 = bf16[4096,1024]{1,0:T(8,128)(2,1)} fusion(bf16[4096,1024]{1,0:T(8,128)(2,1)} %param.4, bf16[4096,4096]{1,0:T(8,128)(2,1)} %all-gather.5.cloned.1.call-done, bf16[1024,4096]{1,0:T(8,128)(2,1)} %param.6), kind=kOutput, calls=%fused_computation.48 | convolution fusion | flops 34389098496 | bytes 58720256 | tf_op jit(solution)/dot_general | solution.py:12
  228.3 43.1 %fusion.37 = bf16[4096,4096]{1,0:T(8,128)(2,1)} fusion(bf16[4096,1024]{1,0:T(8,128)(2,1)} %fusion.34, bf16[4096,1024]{1,0:T(8,128)(2,1)} %param.7), kind=kOutput, calls=%fused_computation.53 | convolution fusion | flops 34359738368 | bytes 50331648 | tf_op jit(solution)/dot_general | solution.py:14
  273.1 9.4 fusion.36
  282.5 11.4 copy.2
  293.8 5.8 collective-permute-done.9
  299.7 607.5 %while.5 = (bf16[1,4096,1024]{1,2,0:T(8,128)(2,1)}, bf16[1,1,256,4096]{3,2,1,0:T(8,128)(2,1)}, f32[1,1024,4096]{2,1,0:T(8,128)}, bf16[1,1,256,4096]{3,2,1,0:T(8,...) while((bf16[1,4096,1024]{1,2,0:T(8,128)(2,1)}, ...), condition=%wide.windowed_dot_general_cond_ag.1.clone, body=%wide.windowed_dot_general_body_ag.1.clone.sunk | while | flops 8610906112 | bytes 134218288 | solution.py:19
  306.6 57.6 %collective-permute-done.4 = bf16[1,1,256,4096]{3,2,1,0:T(8,128)(2,1)} collective-permute-done((bf16[1,1,256,4096]{3,2,1,0:T(8,128)(2,1)S(1)}, bf16[1,1,256,4096]{3,2,1,0:T(8,128)(2,1)}, u32[]{:S(2)}, u32[]{:S(2)}) %collective-permute-start.4) | collective-permute-done | bytes 2097184 | tf_op jit(solution)/gta,gtb->gab/dot_general | solution.py:19
  364.3 4.7 collective-permute-start.5
  368.9 66.3 %collective-permute-done.6 = bf16[1,1,256,4096]{3,2,1,0:T(8,128)(2,1)} collective-permute-done((bf16[1,1,256,4096]{3,2,1,0:T(8,128)(2,1)}, bf16[1,1,256,4096]{3,2,1,0:T(8,128)(2,1)}, u32[]{:S(2)}, u32[]{:S(2)}) %collective-permute-start.6) | collective-permute-done | bytes 2097184 | tf_op jit(solution)/gta,gtb->gab/dot_general | solution.py:19
  435.3 12.3 fusion.53
  448.2 13.0 bitcast_add_fusion.7
  461.2 50.3 %collective-permute-done.7 = bf16[1,1,256,4096]{3,2,1,0:T(8,128)(2,1)} collective-permute-done((bf16[1,1,256,4096]{3,2,1,0:T(8,128)(2,1)}, bf16[1,1,256,4096]{3,2,1,0:T(8,128)(2,1)}, u32[]{:S(2)}, u32[]{:S(2)}) %collective-permute-start.7) | collective-permute-done | bytes 2097184 | tf_op jit(solution)/gta,gtb->gab/dot_general | solution.py:19
  518.4 68.7 %collective-permute-done.4 = bf16[1,1,256,4096]{3,2,1,0:T(8,128)(2,1)} collective-permute-done((bf16[1,1,256,4096]{3,2,1,0:T(8,128)(2,1)S(1)}, bf16[1,1,256,4096]{3,2,1,0:T(8,128)(2,1)}, u32[]{:S(2)}, u32[]{:S(2)}) %collective-permute-start.4) | collective-permute-done | bytes 2097184 | tf_op jit(solution)/gta,gtb->gab/dot_general | solution.py:19
  591.7 11.9 collective-permute-done.6
  603.7 12.3 fusion.53
  616.6 20.8 %bitcast_add_fusion.7 = f32[1,1024,4096]{2,1,0:T(8,128)} fusion(f32[1024,4096,1]{1,0,2:T(8,128)} %fusion.53, f32[1,1024,4096]{2,1,0:T(8,128)} %get-tuple-element.188, pred[]{:T(512)S(6)} %compare.13, bf16[1,1,256,4096]{3,2,1,0:T(8,128)(2,1)} %collective-permute-done.6, bf16[1,1,256,4096]{3,2,1,0:T(8,128)(2,1)} %collective-permute-done.4, ...), kind=kOutput, calls=%fused_computation.25.clone.1 | convolution fusion | flops 4311744512 | bytes 62914568 | tf_op jit(solution)/gta,gtb->gab/dot_general | solution.py:19
  637.4 11.7 collective-permute-done.7
  656.0 63.7 %collective-permute-done.4 = bf16[1,1,256,4096]{3,2,1,0:T(8,128)(2,1)} collective-permute-done((bf16[1,1,256,4096]{3,2,1,0:T(8,128)(2,1)S(1)}, bf16[1,1,256,4096]{3,2,1,0:T(8,128)(2,1)}, u32[]{:S(2)}, u32[]{:S(2)}) %collective-permute-start.4) | collective-permute-done | bytes 2097184 | tf_op jit(solution)/gta,gtb->gab/dot_general | solution.py:19
  724.4 10.6 collective-permute-done.6
  735.0 12.3 fusion.53
  747.9 20.8 %bitcast_add_fusion.7 = f32[1,1024,4096]{2,1,0:T(8,128)} fusion(f32[1024,4096,1]{1,0,2:T(8,128)} %fusion.53, f32[1,1024,4096]{2,1,0:T(8,128)} %get-tuple-element.188, pred[]{:T(512)S(6)} %compare.13, bf16[1,1,256,4096]{3,2,1,0:T(8,128)(2,1)} %collective-permute-done.6, bf16[1,1,256,4096]{3,2,1,0:T(8,128)(2,1)} %collective-permute-done.4, ...), kind=kOutput, calls=%fused_computation.25.clone.1 | convolution fusion | flops 4311744512 | bytes 62914568 | tf_op jit(solution)/gta,gtb->gab/dot_general | solution.py:19
  768.7 38.3 %collective-permute-done.5 = bf16[1,1,256,4096]{3,2,1,0:T(8,128)(2,1)} collective-permute-done((bf16[1,1,256,4096]{3,2,1,0:T(8,128)(2,1)}, bf16[1,1,256,4096]{3,2,1,0:T(8,128)(2,1)}, u32[]{:S(2)}, u32[]{:S(2)}) %collective-permute-start.5) | collective-permute-done | bytes 2097184 | tf_op jit(solution)/gta,gtb->gab/dot_general | solution.py:19
  808.6 4.6 collective-permute-start.4
  818.1 38.7 %collective-permute-done.4 = bf16[1,1,256,4096]{3,2,1,0:T(8,128)(2,1)} collective-permute-done((bf16[1,1,256,4096]{3,2,1,0:T(8,128)(2,1)S(1)}, bf16[1,1,256,4096]{3,2,1,0:T(8,128)(2,1)}, u32[]{:S(2)}, u32[]{:S(2)}) %collective-permute-start.4) | collective-permute-done | bytes 2097184 | tf_op jit(solution)/gta,gtb->gab/dot_general | solution.py:19
  863.6 12.3 fusion.53
  876.5 20.8 %bitcast_add_fusion.7 = f32[1,1024,4096]{2,1,0:T(8,128)} fusion(f32[1024,4096,1]{1,0,2:T(8,128)} %fusion.53, f32[1,1024,4096]{2,1,0:T(8,128)} %get-tuple-element.188, pred[]{:T(512)S(6)} %compare.13, bf16[1,1,256,4096]{3,2,1,0:T(8,128)(2,1)} %collective-permute-done.6, bf16[1,1,256,4096]{3,2,1,0:T(8,128)(2,1)} %collective-permute-done.4, ...), kind=kOutput, calls=%fused_computation.25.clone.1 | convolution fusion | flops 4311744512 | bytes 62914568 | tf_op jit(solution)/gta,gtb->gab/dot_general | solution.py:19
  897.3 9.8 collective-permute-done.5
  907.2 9.0 convert_bitcast_fusion
  916.1 11.3 copy
  927.4 400.8 %while.4 = (bf16[1,4096,1024]{1,2,0:T(8,128)(2,1)}, bf16[1,1,256,4096]{3,2,1,0:T(8,128)(2,1)}, f32[1,1024,4096]{2,1,0:T(8,128)}, bf16[1,1,256,4096]{3,2,1,0:T(8,...) while((bf16[1,4096,1024]{1,2,0:T(8,128)(2,1)}, ...), condition=%wide.windowed_dot_general_cond_ag.clone, body=%wide.windowed_dot_general_body_ag.clone.sunk | while | flops 8610906112 | bytes 134218288 | solution.py:19
  938.6 40.8 %collective-permute-done = bf16[1,1,256,4096]{3,2,1,0:T(8,128)(2,1)} collective-permute-done((bf16[1,1,256,4096]{3,2,1,0:T(8,128)(2,1)S(1)}, bf16[1,1,256,4096]{3,2,1,0:T(8,128)(2,1)}, u32[]{:S(2)}, u32[]{:S(2)}) %collective-permute-start) | collective-permute-done | bytes 2097184 | tf_op jit(solution)/gta,gtb->gab/dot_general | solution.py:19
  984.1 12.2 fusion.50
  996.9 13.0 bitcast_add_fusion.6
  1009.9 17.7 %collective-permute-done.1 = bf16[1,1,256,4096]{3,2,1,0:T(8,128)(2,1)} collective-permute-done((bf16[1,1,256,4096]{3,2,1,0:T(8,128)(2,1)}, bf16[1,1,256,4096]{3,2,1,0:T(8,128)(2,1)}, u32[]{:S(2)}, u32[]{:S(2)}) %collective-permute-start.1) | collective-permute-done | bytes 2097184 | tf_op jit(solution)/gta,gtb->gab/dot_general | solution.py:19
  1038.8 39.4 %collective-permute-done = bf16[1,1,256,4096]{3,2,1,0:T(8,128)(2,1)} collective-permute-done((bf16[1,1,256,4096]{3,2,1,0:T(8,128)(2,1)S(1)}, bf16[1,1,256,4096]{3,2,1,0:T(8,128)(2,1)}, u32[]{:S(2)}, u32[]{:S(2)}) %collective-permute-start) | collective-permute-done | bytes 2097184 | tf_op jit(solution)/gta,gtb->gab/dot_general | solution.py:19
  1084.2 12.2 fusion.50
  1097.0 20.8 %bitcast_add_fusion.6 = f32[1,1024,4096]{2,1,0:T(8,128)} fusion(f32[1024,4096,1]{1,0,2:T(8,128)} %fusion.50, f32[1,1024,4096]{2,1,0:T(8,128)} %get-tuple-element.155, pred[]{:T(512)S(6)} %compare.12, bf16[1,1,256,4096]{3,2,1,0:T(8,128)(2,1)} %collective-permute-done.2, bf16[1,1,256,4096]{3,2,1,0:T(8,128)(2,1)} %collective-permute-done, ...), kind=kOutput, calls=%fused_computation.4.clone.1 | convolution fusion | flops 4311744512 | bytes 62914568 | tf_op jit(solution)/gta,gtb->gab/dot_general | solution.py:19
  1117.8 6.6 collective-permute-done.1
  1135.6 39.4 %collective-permute-done = bf16[1,1,256,4096]{3,2,1,0:T(8,128)(2,1)} collective-permute-done((bf16[1,1,256,4096]{3,2,1,0:T(8,128)(2,1)S(1)}, bf16[1,1,256,4096]{3,2,1,0:T(8,128)(2,1)}, u32[]{:S(2)}, u32[]{:S(2)}) %collective-permute-start) | collective-permute-done | bytes 2097184 | tf_op jit(solution)/gta,gtb->gab/dot_general | solution.py:19
  1183.8 12.2 fusion.50
  1196.7 20.8 %bitcast_add_fusion.6 = f32[1,1024,4096]{2,1,0:T(8,128)} fusion(f32[1024,4096,1]{1,0,2:T(8,128)} %fusion.50, f32[1,1024,4096]{2,1,0:T(8,128)} %get-tuple-element.155, pred[]{:T(512)S(6)} %compare.12, bf16[1,1,256,4096]{3,2,1,0:T(8,128)(2,1)} %collective-permute-done.2, bf16[1,1,256,4096]{3,2,1,0:T(8,128)(2,1)} %collective-permute-done, ...), kind=kOutput, calls=%fused_computation.4.clone.1 | convolution fusion | flops 4311744512 | bytes 62914568 | tf_op jit(solution)/gta,gtb->gab/dot_general | solution.py:19
  1221.2 8.0 collective-permute-done.3
  1236.3 37.6 %collective-permute-done = bf16[1,1,256,4096]{3,2,1,0:T(8,128)(2,1)} collective-permute-done((bf16[1,1,256,4096]{3,2,1,0:T(8,128)(2,1)S(1)}, bf16[1,1,256,4096]{3,2,1,0:T(8,128)(2,1)}, u32[]{:S(2)}, u32[]{:S(2)}) %collective-permute-start) | collective-permute-done | bytes 2097184 | tf_op jit(solution)/gta,gtb->gab/dot_general | solution.py:19
  1282.9 12.2 fusion.50
  1295.7 20.8 %bitcast_add_fusion.6 = f32[1,1024,4096]{2,1,0:T(8,128)} fusion(f32[1024,4096,1]{1,0,2:T(8,128)} %fusion.50, f32[1,1024,4096]{2,1,0:T(8,128)} %get-tuple-element.155, pred[]{:T(512)S(6)} %compare.12, bf16[1,1,256,4096]{3,2,1,0:T(8,128)(2,1)} %collective-permute-done.2, bf16[1,1,256,4096]{3,2,1,0:T(8,128)(2,1)} %collective-permute-done, ...), kind=kOutput, calls=%fused_computation.4.clone.1 | convolution fusion | flops 4311744512 | bytes 62914568 | tf_op jit(solution)/gta,gtb->gab/dot_general | solution.py:19
  1316.5 7.8 collective-permute-done.1
  1328.3 13.8 %copy.1 = bf16[1,1024,4096]{1,2,0:T(8,128)(2,1)} copy(f32[1,1024,4096]{2,1,0:T(8,128)} %get-tuple-element.12) | data formatting | bytes 25165824 | tf_op jit(solution)/gta,gtb->gab/dot_general | solution.py:19
  (81 shorter events, 119.0 us)
Async XLA Ops:
  7.2 177.3 %all-gather.5.cloned.1.call-start = ((), (), s32[]{:S(2)}) async-start(), calls=%async_computation.1 | async-start | bytes 35651584 | tf_op args[1]
  13.6 1328.5 %reduce-scatter.4.cloned.1.call-start = ((), (), s32[]{:S(2)}) async-start(), calls=%async_computation.2 | async-start | bytes 35651584
  271.4 28.2 %collective-permute-start.9 = (bf16[1,1,256,4096]{3,2,1,0:T(8,128)(2,1)}, bf16[1,1,256,4096]{3,2,1,0:T(8,128)(2,1)}, u32[]{:S(2)}, u32[]{:S(2)}) collective-permute-start(bf16[1,1,256,4096]{3,2,1,0:T(8,128)(2,1)} %bitcast.6), channel_id=11, source_target_pairs={{0,1},{1,2},{2,3},{3,4},{4,5},{5,6},{6,7},{7,8},{8,9},{9,10},{10,1... | collective-permute-start | bytes 6291464 | tf_op jit(solution)/gta,gtb->gab/dot_general | solution.py:19
  271.8 655.7 %collective-permute-start.8 = (bf16[1,1,256,4096]{3,2,1,0:T(8,128)(2,1)}, bf16[1,1,256,4096]{3,2,1,0:T(8,128)(2,1)}, u32[]{:S(2)}, u32[]{:S(2)}) collective-permute-start(bf16[1,1,256,4096]{3,2,1,0:T(8,128)(2,1)} %bitcast.2), channel_id=5, source_target_pairs={{0,1},{1,2},{2,3},{3,4},{4,5},{5,6},{6,7},{7,8},{8,9},{9,10},{10,1... | collective-permute-start | bytes 6291464 | tf_op jit(solution)/gta,gtb->gab/dot_general | solution.py:19
  282.5 17.2 %copy-start = (u32[32]{0:T(128)S(1)}, u32[32]{0:T(128)}, u32[]{:S(2)}) copy-start(u32[32]{0:T(128)} %constant.230) | copy-start | bytes 388
  301.3 63.0 %collective-permute-start.4 = (bf16[1,1,256,4096]{3,2,1,0:T(8,128)(2,1)S(1)}, bf16[1,1,256,4096]{3,2,1,0:T(8,128)(2,1)}, u32[]{:S(2)}, u32[]{:S(2)}) collective-permute-start(bf16[1,1,256,4096]{3,2,1,0:T(8,128)(2,1)S(1)} %copy.19), channel_id=12, source_target_pairs={{0,15},{1,0},{2,1},{3,2},{4,3},{5,4},{6,5},{7,6},{8,7},{9,8},{10,9... | collective-permute-start | bytes 6291464 | tf_op jit(solution)/gta,gtb->gab/dot_general | solution.py:19
  304.4 130.9 %collective-permute-start.6 = (bf16[1,1,256,4096]{3,2,1,0:T(8,128)(2,1)}, bf16[1,1,256,4096]{3,2,1,0:T(8,128)(2,1)}, u32[]{:S(2)}, u32[]{:S(2)}) collective-permute-start(bf16[1,1,256,4096]{3,2,1,0:T(8,128)(2,1)} %copy.21), channel_id=13, source_target_pairs={{0,1},{1,2},{2,3},{3,4},{4,5},{5,6},{6,7},{7,8},{8,9},{9,10},{10,1... | collective-permute-start | bytes 6291464 | tf_op jit(solution)/gta,gtb->gab/dot_general | solution.py:19
  364.3 96.9 %collective-permute-start.5 = (bf16[1,1,256,4096]{3,2,1,0:T(8,128)(2,1)}, bf16[1,1,256,4096]{3,2,1,0:T(8,128)(2,1)}, u32[]{:S(2)}, u32[]{:S(2)}) collective-permute-start(bf16[1,1,256,4096]{3,2,1,0:T(8,128)(2,1)} %collective-permute-done.4), channel_id=14, source_target_pairs={{0,15},{1,0},{2,1},{3,2},{4,3},{5,4},{6,5},{7,6},{8,7},{9,8},{10,9... | collective-permute-start | bytes 6291464 | tf_op jit(solution)/gta,gtb->gab/dot_general | solution.py:19
  435.3 76.2 %collective-permute-start.7 = (bf16[1,1,256,4096]{3,2,1,0:T(8,128)(2,1)}, bf16[1,1,256,4096]{3,2,1,0:T(8,128)(2,1)}, u32[]{:S(2)}, u32[]{:S(2)}) collective-permute-start(bf16[1,1,256,4096]{3,2,1,0:T(8,128)(2,1)} %collective-permute-done.6), channel_id=15, source_target_pairs={{0,1},{1,2},{2,3},{3,4},{4,5},{5,6},{6,7},{7,8},{8,9},{9,10},{10,1... | collective-permute-start | bytes 6291464 | tf_op jit(solution)/gta,gtb->gab/dot_general | solution.py:19
  513.0 74.1 %collective-permute-start.4 = (bf16[1,1,256,4096]{3,2,1,0:T(8,128)(2,1)S(1)}, bf16[1,1,256,4096]{3,2,1,0:T(8,128)(2,1)}, u32[]{:S(2)}, u32[]{:S(2)}) collective-permute-start(bf16[1,1,256,4096]{3,2,1,0:T(8,128)(2,1)S(1)} %copy.19), channel_id=12, source_target_pairs={{0,15},{1,0},{2,1},{3,2},{4,3},{5,4},{6,5},{7,6},{8,7},{9,8},{10,9... | collective-permute-start | bytes 6291464 | tf_op jit(solution)/gta,gtb->gab/dot_general | solution.py:19
  516.2 87.5 %collective-permute-start.6 = (bf16[1,1,256,4096]{3,2,1,0:T(8,128)(2,1)}, bf16[1,1,256,4096]{3,2,1,0:T(8,128)(2,1)}, u32[]{:S(2)}, u32[]{:S(2)}) collective-permute-start(bf16[1,1,256,4096]{3,2,1,0:T(8,128)(2,1)} %copy.21), channel_id=13, source_target_pairs={{0,1},{1,2},{2,3},{3,4},{4,5},{5,6},{6,7},{7,8},{8,9},{9,10},{10,1... | collective-permute-start | bytes 6291464 | tf_op jit(solution)/gta,gtb->gab/dot_general | solution.py:19
  587.1 50.3 %collective-permute-start.5 = (bf16[1,1,256,4096]{3,2,1,0:T(8,128)(2,1)}, bf16[1,1,256,4096]{3,2,1,0:T(8,128)(2,1)}, u32[]{:S(2)}, u32[]{:S(2)}) collective-permute-start(bf16[1,1,256,4096]{3,2,1,0:T(8,128)(2,1)} %collective-permute-done.4), channel_id=14, source_target_pairs={{0,15},{1,0},{2,1},{3,2},{4,3},{5,4},{6,5},{7,6},{8,7},{9,8},{10,9... | collective-permute-start | bytes 6291464 | tf_op jit(solution)/gta,gtb->gab/dot_general | solution.py:19
  603.7 45.4 %collective-permute-start.7 = (bf16[1,1,256,4096]{3,2,1,0:T(8,128)(2,1)}, bf16[1,1,256,4096]{3,2,1,0:T(8,128)(2,1)}, u32[]{:S(2)}, u32[]{:S(2)}) collective-permute-start(bf16[1,1,256,4096]{3,2,1,0:T(8,128)(2,1)} %collective-permute-done.6), channel_id=15, source_target_pairs={{0,1},{1,2},{2,3},{3,4},{4,5},{5,6},{6,7},{7,8},{8,9},{9,10},{10,1... | collective-permute-start | bytes 6291464 | tf_op jit(solution)/gta,gtb->gab/dot_general | solution.py:19
  650.7 69.1 %collective-permute-start.4 = (bf16[1,1,256,4096]{3,2,1,0:T(8,128)(2,1)S(1)}, bf16[1,1,256,4096]{3,2,1,0:T(8,128)(2,1)}, u32[]{:S(2)}, u32[]{:S(2)}) collective-permute-start(bf16[1,1,256,4096]{3,2,1,0:T(8,128)(2,1)S(1)} %copy.19), channel_id=12, source_target_pairs={{0,15},{1,0},{2,1},{3,2},{4,3},{5,4},{6,5},{7,6},{8,7},{9,8},{10,9... | collective-permute-start | bytes 6291464 | tf_op jit(solution)/gta,gtb->gab/dot_general | solution.py:19
  653.8 81.2 %collective-permute-start.6 = (bf16[1,1,256,4096]{3,2,1,0:T(8,128)(2,1)}, bf16[1,1,256,4096]{3,2,1,0:T(8,128)(2,1)}, u32[]{:S(2)}, u32[]{:S(2)}) collective-permute-start(bf16[1,1,256,4096]{3,2,1,0:T(8,128)(2,1)} %copy.21), channel_id=13, source_target_pairs={{0,1},{1,2},{2,3},{3,4},{4,5},{5,6},{6,7},{7,8},{8,9},{9,10},{10,1... | collective-permute-start | bytes 6291464 | tf_op jit(solution)/gta,gtb->gab/dot_general | solution.py:19
  719.8 87.2 %collective-permute-start.5 = (bf16[1,1,256,4096]{3,2,1,0:T(8,128)(2,1)}, bf16[1,1,256,4096]{3,2,1,0:T(8,128)(2,1)}, u32[]{:S(2)}, u32[]{:S(2)}) collective-permute-start(bf16[1,1,256,4096]{3,2,1,0:T(8,128)(2,1)} %collective-permute-done.4), channel_id=14, source_target_pairs={{0,15},{1,0},{2,1},{3,2},{4,3},{5,4},{6,5},{7,6},{8,7},{9,8},{10,9... | collective-permute-start | bytes 6291464 | tf_op jit(solution)/gta,gtb->gab/dot_general | solution.py:19
  735.0 72.0 %collective-permute-start.7 = (bf16[1,1,256,4096]{3,2,1,0:T(8,128)(2,1)}, bf16[1,1,256,4096]{3,2,1,0:T(8,128)(2,1)}, u32[]{:S(2)}, u32[]{:S(2)}) collective-permute-start(bf16[1,1,256,4096]{3,2,1,0:T(8,128)(2,1)} %collective-permute-done.6), channel_id=15, source_target_pairs={{0,1},{1,2},{2,3},{3,4},{4,5},{5,6},{6,7},{7,8},{8,9},{9,10},{10,1... | collective-permute-start | bytes 6291464 | tf_op jit(solution)/gta,gtb->gab/dot_general | solution.py:19
  808.6 48.2 %collective-permute-start.4 = (bf16[1,1,256,4096]{3,2,1,0:T(8,128)(2,1)S(1)}, bf16[1,1,256,4096]{3,2,1,0:T(8,128)(2,1)}, u32[]{:S(2)}, u32[]{:S(2)}) collective-permute-start(bf16[1,1,256,4096]{3,2,1,0:T(8,128)(2,1)S(1)} %copy.19), channel_id=12, source_target_pairs={{0,15},{1,0},{2,1},{3,2},{4,3},{5,4},{6,5},{7,6},{8,7},{9,8},{10,9... | collective-permute-start | bytes 6291464 | tf_op jit(solution)/gta,gtb->gab/dot_general | solution.py:19
  816.4 47.3 %collective-permute-start.6 = (bf16[1,1,256,4096]{3,2,1,0:T(8,128)(2,1)}, bf16[1,1,256,4096]{3,2,1,0:T(8,128)(2,1)}, u32[]{:S(2)}, u32[]{:S(2)}) collective-permute-start(bf16[1,1,256,4096]{3,2,1,0:T(8,128)(2,1)} %copy.21), channel_id=13, source_target_pairs={{0,1},{1,2},{2,3},{3,4},{4,5},{5,6},{6,7},{7,8},{8,9},{9,10},{10,1... | collective-permute-start | bytes 6291464 | tf_op jit(solution)/gta,gtb->gab/dot_general | solution.py:19
  856.8 50.4 %collective-permute-start.5 = (bf16[1,1,256,4096]{3,2,1,0:T(8,128)(2,1)}, bf16[1,1,256,4096]{3,2,1,0:T(8,128)(2,1)}, u32[]{:S(2)}, u32[]{:S(2)}) collective-permute-start(bf16[1,1,256,4096]{3,2,1,0:T(8,128)(2,1)} %collective-permute-done.4), channel_id=14, source_target_pairs={{0,15},{1,0},{2,1},{3,2},{4,3},{5,4},{6,5},{7,6},{8,7},{9,8},{10,9... | collective-permute-start | bytes 6291464 | tf_op jit(solution)/gta,gtb->gab/dot_general | solution.py:19
  863.6 43.5 %collective-permute-start.7 = (bf16[1,1,256,4096]{3,2,1,0:T(8,128)(2,1)}, bf16[1,1,256,4096]{3,2,1,0:T(8,128)(2,1)}, u32[]{:S(2)}, u32[]{:S(2)}) collective-permute-start(bf16[1,1,256,4096]{3,2,1,0:T(8,128)(2,1)} %collective-permute-done.6), channel_id=15, source_target_pairs={{0,1},{1,2},{2,3},{3,4},{4,5},{5,6},{6,7},{7,8},{8,9},{9,10},{10,1... | collective-permute-start | bytes 6291464 | tf_op jit(solution)/gta,gtb->gab/dot_general | solution.py:19
  929.0 50.4 %collective-permute-start = (bf16[1,1,256,4096]{3,2,1,0:T(8,128)(2,1)S(1)}, bf16[1,1,256,4096]{3,2,1,0:T(8,128)(2,1)}, u32[]{:S(2)}, u32[]{:S(2)}) collective-permute-start(bf16[1,1,256,4096]{3,2,1,0:T(8,128)(2,1)S(1)} %copy.7), channel_id=6, source_target_pairs={{0,15},{1,0},{2,1},{3,2},{4,3},{5,4},{6,5},{7,6},{8,7},{9,8},{10,9... | collective-permute-start | bytes 6291464 | tf_op jit(solution)/gta,gtb->gab/dot_general | solution.py:19
  936.8 47.3 %collective-permute-start.2 = (bf16[1,1,256,4096]{3,2,1,0:T(8,128)(2,1)}, bf16[1,1,256,4096]{3,2,1,0:T(8,128)(2,1)}, u32[]{:S(2)}, u32[]{:S(2)}) collective-permute-start(bf16[1,1,256,4096]{3,2,1,0:T(8,128)(2,1)} %copy.9), channel_id=7, source_target_pairs={{0,1},{1,2},{2,3},{3,4},{4,5},{5,6},{6,7},{7,8},{8,9},{9,10},{10,1... | collective-permute-start | bytes 6291464 | tf_op jit(solution)/gta,gtb->gab/dot_general | solution.py:19
  979.4 48.1 %collective-permute-start.1 = (bf16[1,1,256,4096]{3,2,1,0:T(8,128)(2,1)}, bf16[1,1,256,4096]{3,2,1,0:T(8,128)(2,1)}, u32[]{:S(2)}, u32[]{:S(2)}) collective-permute-start(bf16[1,1,256,4096]{3,2,1,0:T(8,128)(2,1)} %collective-permute-done), channel_id=8, source_target_pairs={{0,15},{1,0},{2,1},{3,2},{4,3},{5,4},{6,5},{7,6},{8,7},{9,8},{10,9... | collective-permute-start | bytes 6291464 | tf_op jit(solution)/gta,gtb->gab/dot_general | solution.py:19
  984.1 43.5 %collective-permute-start.3 = (bf16[1,1,256,4096]{3,2,1,0:T(8,128)(2,1)}, bf16[1,1,256,4096]{3,2,1,0:T(8,128)(2,1)}, u32[]{:S(2)}, u32[]{:S(2)}) collective-permute-start(bf16[1,1,256,4096]{3,2,1,0:T(8,128)(2,1)} %collective-permute-done.2), channel_id=9, source_target_pairs={{0,1},{1,2},{2,3},{3,4},{4,5},{5,6},{6,7},{7,8},{8,9},{9,10},{10,1... | collective-permute-start | bytes 6291464 | tf_op jit(solution)/gta,gtb->gab/dot_general | solution.py:19
  1029.2 49.0 %collective-permute-start = (bf16[1,1,256,4096]{3,2,1,0:T(8,128)(2,1)S(1)}, bf16[1,1,256,4096]{3,2,1,0:T(8,128)(2,1)}, u32[]{:S(2)}, u32[]{:S(2)}) collective-permute-start(bf16[1,1,256,4096]{3,2,1,0:T(8,128)(2,1)S(1)} %copy.7), channel_id=6, source_target_pairs={{0,15},{1,0},{2,1},{3,2},{4,3},{5,4},{6,5},{7,6},{8,7},{9,8},{10,9... | collective-permute-start | bytes 6291464 | tf_op jit(solution)/gta,gtb->gab/dot_general | solution.py:19
  1036.9 47.3 %collective-permute-start.2 = (bf16[1,1,256,4096]{3,2,1,0:T(8,128)(2,1)}, bf16[1,1,256,4096]{3,2,1,0:T(8,128)(2,1)}, u32[]{:S(2)}, u32[]{:S(2)}) collective-permute-start(bf16[1,1,256,4096]{3,2,1,0:T(8,128)(2,1)} %copy.9), channel_id=7, source_target_pairs={{0,1},{1,2},{2,3},{3,4},{4,5},{5,6},{6,7},{7,8},{8,9},{9,10},{10,1... | collective-permute-start | bytes 6291464 | tf_op jit(solution)/gta,gtb->gab/dot_general | solution.py:19
  1078.1 46.3 %collective-permute-start.1 = (bf16[1,1,256,4096]{3,2,1,0:T(8,128)(2,1)}, bf16[1,1,256,4096]{3,2,1,0:T(8,128)(2,1)}, u32[]{:S(2)}, u32[]{:S(2)}) collective-permute-start(bf16[1,1,256,4096]{3,2,1,0:T(8,128)(2,1)} %collective-permute-done), channel_id=8, source_target_pairs={{0,15},{1,0},{2,1},{3,2},{4,3},{5,4},{6,5},{7,6},{8,7},{9,8},{10,9... | collective-permute-start | bytes 6291464 | tf_op jit(solution)/gta,gtb->gab/dot_general | solution.py:19
  1084.2 40.2 %collective-permute-start.3 = (bf16[1,1,256,4096]{3,2,1,0:T(8,128)(2,1)}, bf16[1,1,256,4096]{3,2,1,0:T(8,128)(2,1)}, u32[]{:S(2)}, u32[]{:S(2)}) collective-permute-start(bf16[1,1,256,4096]{3,2,1,0:T(8,128)(2,1)} %collective-permute-done.2), channel_id=9, source_target_pairs={{0,1},{1,2},{2,3},{3,4},{4,5},{5,6},{6,7},{7,8},{8,9},{9,10},{10,1... | collective-permute-start | bytes 6291464 | tf_op jit(solution)/gta,gtb->gab/dot_general | solution.py:19
  1126.0 49.0 %collective-permute-start = (bf16[1,1,256,4096]{3,2,1,0:T(8,128)(2,1)S(1)}, bf16[1,1,256,4096]{3,2,1,0:T(8,128)(2,1)}, u32[]{:S(2)}, u32[]{:S(2)}) collective-permute-start(bf16[1,1,256,4096]{3,2,1,0:T(8,128)(2,1)S(1)} %copy.7), channel_id=6, source_target_pairs={{0,15},{1,0},{2,1},{3,2},{4,3},{5,4},{6,5},{7,6},{8,7},{9,8},{10,9... | collective-permute-start | bytes 6291464 | tf_op jit(solution)/gta,gtb->gab/dot_general | solution.py:19
  1133.8 50.1 %collective-permute-start.2 = (bf16[1,1,256,4096]{3,2,1,0:T(8,128)(2,1)}, bf16[1,1,256,4096]{3,2,1,0:T(8,128)(2,1)}, u32[]{:S(2)}, u32[]{:S(2)}) collective-permute-start(bf16[1,1,256,4096]{3,2,1,0:T(8,128)(2,1)} %copy.9), channel_id=7, source_target_pairs={{0,1},{1,2},{2,3},{3,4},{4,5},{5,6},{6,7},{7,8},{8,9},{9,10},{10,1... | collective-permute-start | bytes 6291464 | tf_op jit(solution)/gta,gtb->gab/dot_general | solution.py:19
  1175.0 46.3 %collective-permute-start.1 = (bf16[1,1,256,4096]{3,2,1,0:T(8,128)(2,1)}, bf16[1,1,256,4096]{3,2,1,0:T(8,128)(2,1)}, u32[]{:S(2)}, u32[]{:S(2)}) collective-permute-start(bf16[1,1,256,4096]{3,2,1,0:T(8,128)(2,1)} %collective-permute-done), channel_id=8, source_target_pairs={{0,15},{1,0},{2,1},{3,2},{4,3},{5,4},{6,5},{7,6},{8,7},{9,8},{10,9... | collective-permute-start | bytes 6291464 | tf_op jit(solution)/gta,gtb->gab/dot_general | solution.py:19
  1183.8 45.4 %collective-permute-start.3 = (bf16[1,1,256,4096]{3,2,1,0:T(8,128)(2,1)}, bf16[1,1,256,4096]{3,2,1,0:T(8,128)(2,1)}, u32[]{:S(2)}, u32[]{:S(2)}) collective-permute-start(bf16[1,1,256,4096]{3,2,1,0:T(8,128)(2,1)} %collective-permute-done.2), channel_id=9, source_target_pairs={{0,1},{1,2},{2,3},{3,4},{4,5},{5,6},{6,7},{7,8},{8,9},{9,10},{10,1... | collective-permute-start | bytes 6291464 | tf_op jit(solution)/gta,gtb->gab/dot_general | solution.py:19
  1230.8 43.1 %collective-permute-start = (bf16[1,1,256,4096]{3,2,1,0:T(8,128)(2,1)S(1)}, bf16[1,1,256,4096]{3,2,1,0:T(8,128)(2,1)}, u32[]{:S(2)}, u32[]{:S(2)}) collective-permute-start(bf16[1,1,256,4096]{3,2,1,0:T(8,128)(2,1)S(1)} %copy.7), channel_id=6, source_target_pairs={{0,15},{1,0},{2,1},{3,2},{4,3},{5,4},{6,5},{7,6},{8,7},{9,8},{10,9... | collective-permute-start | bytes 6291464 | tf_op jit(solution)/gta,gtb->gab/dot_general | solution.py:19
  1233.9 49.0 %collective-permute-start.2 = (bf16[1,1,256,4096]{3,2,1,0:T(8,128)(2,1)}, bf16[1,1,256,4096]{3,2,1,0:T(8,128)(2,1)}, u32[]{:S(2)}, u32[]{:S(2)}) collective-permute-start(bf16[1,1,256,4096]{3,2,1,0:T(8,128)(2,1)} %copy.9), channel_id=7, source_target_pairs={{0,1},{1,2},{2,3},{3,4},{4,5},{5,6},{6,7},{7,8},{8,9},{9,10},{10,1... | collective-permute-start | bytes 6291464 | tf_op jit(solution)/gta,gtb->gab/dot_general | solution.py:19
  1273.9 50.4 %collective-permute-start.1 = (bf16[1,1,256,4096]{3,2,1,0:T(8,128)(2,1)}, bf16[1,1,256,4096]{3,2,1,0:T(8,128)(2,1)}, u32[]{:S(2)}, u32[]{:S(2)}) collective-permute-start(bf16[1,1,256,4096]{3,2,1,0:T(8,128)(2,1)} %collective-permute-done), channel_id=8, source_target_pairs={{0,15},{1,0},{2,1},{3,2},{4,3},{5,4},{6,5},{7,6},{8,7},{9,8},{10,9... | collective-permute-start | bytes 6291464 | tf_op jit(solution)/gta,gtb->gab/dot_general | solution.py:19
  1282.9 45.4 %collective-permute-start.3 = (bf16[1,1,256,4096]{3,2,1,0:T(8,128)(2,1)}, bf16[1,1,256,4096]{3,2,1,0:T(8,128)(2,1)}, u32[]{:S(2)}, u32[]{:S(2)}) collective-permute-start(bf16[1,1,256,4096]{3,2,1,0:T(8,128)(2,1)} %collective-permute-done.2), channel_id=9, source_target_pairs={{0,1},{1,2},{2,3},{3,4},{4,5},{5,6},{6,7},{7,8},{8,9},{9,10},{10,1... | collective-permute-start | bytes 6291464 | tf_op jit(solution)/gta,gtb->gab/dot_general | solution.py:19
Sparse Core Ops, SparseCore 0:
  13.7 170.6 all-gather.4
  271.6 529.6 reduce-scatter.3
where the time goes:
time: 1350 us
  waiting for transfers between devices  822 us (61%)
  matrix products  336 us (25%)
  local copies, waits for them, and re-layouts  85.3 us (6%)
  starting transfers between devices  59.3 us (4%)
  other arithmetic  18.3 us (1%)
  loops' own time  14.5 us (1%)
  between operations  14 us (1%)
    dot_general x34, waiting for transfers between devices, by_group(): jnp.einsum('gta,gtb->gab', a, b, preferred_element_type=jnp.float32)  651 us
    dot_general x16, matrix products, by_group(): jnp.einsum('gta,gtb->gab', a, b, preferred_element_type=jnp.float32)  249 us
    unnamed x4, waiting for transfers between devices  171 us
    dot_general x34, starting transfers between devices, by_group(): jnp.einsum('gta,gtb->gab', a, b, preferred_element_type=jnp.float32)  59.3 us
    dot_general x1, matrix products, step(): d_hidden = jnp.dot(dy, w_down.T, preferred_element_type=jnp.float32)  43.9 us
    dot_general x1, matrix products, step(): dx = jnp.dot(d_pre, w_in.T)  43.1 us
    dot_general x16, local copies, waits for them, and re-layouts  37.8 us
    unnamed x6, local copies, waits for them, and re-layouts  29 us
  transfers between devices with their start and end apart: 36, of which 27 were waited for; matrix products, arithmetic and copies ran while one was open for 26% of the time, Pallas kernels for 0%

commit v1 on v0

v1 whole, which is shorter than its diff:
```python
import jax
import jax.numpy as jnp
from jax import lax
from jax.sharding import PartitionSpec as P


def act(pre):
    return jnp.square(jax.nn.relu(pre))


def over_tokens(a, b):
    return lax.dot_general(a, b, (((0,), (0,)), ((), ())), preferred_element_type=jnp.float32)


def solution(mesh):
    def step(x, dy, pre, w_in, w_down):
        dy = lax.all_gather(dy, "tp", tiled=True)
        x = lax.all_gather(x, "tp", tiled=True)
        hidden, back = jax.vjp(act, pre.astype(jnp.float32))
        d_hidden = jnp.dot(dy, w_down.T, preferred_element_type=jnp.float32)
        d_pre = back(d_hidden)[0].astype(jnp.bfloat16)
        dx = jnp.dot(d_pre, w_in.T, preferred_element_type=jnp.float32).astype(jnp.bfloat16)
        dx = lax.psum_scatter(dx, "tp", scatter_dimension=0, tiled=True)
        dw_down = over_tokens(hidden.astype(jnp.bfloat16), dy).astype(jnp.bfloat16)
        dw_in = over_tokens(x, d_pre).astype(jnp.bfloat16)
        return dx, dw_in, dw_down

    rows = P(("dp", "tp"), None)
    return jax.shard_map(
        step,
        mesh=mesh,
        in_specs=(rows, rows, P("dp", "tp"), P(None, "tp"), P("tp", None)),
        out_specs=(rows, P("dp", "tp"), rows),
        check_vma=False,
    )
```

time: 1350 us -> 690 us (0.51)
  waiting for transfers between devices: 822 us -> 490 us
  matrix products: 336 us -> 173 us
  local copies, waits for them, and re-layouts: 85.3 us -> 11.9 us
  starting transfers between devices: 59.3 us -> 0.11 us
  other arithmetic: 18.3 us -> 0 us
  loops' own time: 14.5 us -> 0 us
    dot_general x34 -> x0, waiting for transfers between devices: 651 us -> none  [by_group(): jnp.einsum('gta,gtb->gab', a, b, preferred_element_type=jnp.float32)]
    all_gather x0 -> x2, waiting for transfers between devices: none -> 254 us  [the longest x1 172 us: step(): dy = lax.all_gather(dy, 'tp', tiled=True)]
    reduce_scatter x0 -> x1, waiting for transfers between devices: none -> 235 us  [step(): dx = lax.psum_scatter(dx, 'tp', scatter_dimension=0, tiled=True)]
    unnamed x4 -> x3, waiting for transfers between devices: 171 us -> 1.39 us
    dot_general x17 -> x3, matrix products: 292 us -> 129 us  [the longest x2 86.3 us: over_tokens(): lax.dot_general(a, b, (((0,), (0,)), ((), ())), preferred_element_type=jn...]
    dot_general x34 -> x0, starting transfers between devices: 59.3 us -> none  [by_group(): jnp.einsum('gta,gtb->gab', a, b, preferred_element_type=jnp.float32)]
    dot_general x25 -> x0, local copies, waits for them, and re-layouts: 56.3 us -> none
    reshape x2 -> x0, other arithmetic: 18.3 us -> none  [the longest x1 9.36 us: by_group(): a, b = (t.reshape(groups, -1, t.shape[-1]) for t in (a, b))]
  transfers between devices with their start and end apart: 36 -> 3, of which waited for: 27 -> 3; matrix products, arithmetic and copies ran while one was open for 26% -> 27% of each run, Pallas kernels for 0% -> 0%
where the time goes in v1:
time: 690 us; the launch traced here: 689 us
  waiting for transfers between devices  490 us (71%)
  matrix products  173 us (25%)
  between operations  13.7 us (2%)
  local copies, waits for them, and re-layouts  11.9 us (2%)
    reduce_scatter x1, waiting for transfers between devices, step(): dx = lax.psum_scatter(dx, 'tp', scatter_dimension=0, tiled=True)  235 us
    all_gather x1, waiting for transfers between devices, step(): dy = lax.all_gather(dy, 'tp', tiled=True)  172 us
    dot_general x2, matrix products, over_tokens(): lax.dot_general(a, b, (((0,), (0,)), ((), ())), preferred_element_type=jn...  86.3 us
    all_gather x1, waiting for transfers between devices, step(): x = lax.all_gather(x, 'tp', tiled=True)  82.6 us
    dot_general x1, matrix products, step(): d_hidden = jnp.dot(dy, w_down.T, preferred_element_type=jnp.float32)  43.9 us
    dot_general x1, matrix products, step(): jnp.dot(d_pre, w_in.T, preferred_element_type=jnp.float32)  43 us
  transfers between devices with their start and end apart: 3, of which 3 were waited for; matrix products, arithmetic and copies ran while one was open for 27% of the time, Pallas kernels for 0%

profile of v1, /device:TPU:0, one launch (start us, length us, event | category | flops | bytes accessed | tf_op | source)
XLA Modules:
  0.0 689.3 jit_solution(3412285343548303977)
XLA Ops:
  7.2 0.0 all-gather.3.cloned.1.call-start
  7.2 0.7 all-gather.3.cloned.1.call-update
  7.9 0.0 all-gather.5.cloned.1.call-start
  7.9 0.7 all-gather.5.cloned.1.call-update
  8.6 0.0 reduce-scatter.2.cloned.1.call-start
  8.7 171.6 %all-gather.3.cloned.1.call-done = bf16[4096,4096]{1,0:T(8,128)(2,1)} async-done(((bf16[256,4096]{1,0:T(8,128)(2,1)}), bf16[4096,4096]{1,0:T(8,128)(2,1)}) %all-gather.3.cloned.1.call-update) | async-done | bytes 33554448 | tf_op jit(solution)/shard_map/all_gather | solution.py:17
  180.3 43.9 %fusion.4 = bf16[4096,1024]{1,0:T(8,128)(2,1)} fusion(bf16[4096,1024]{1,0:T(8,128)(2,1)} %param.7, bf16[4096,4096]{1,0:T(8,128)(2,1)} %all-gather.3.cloned.1.call-done, bf16[1024,4096]{1,0:T(8,128)(2,1)} %param.9), kind=kOutput, calls=%fused_computation.7 | convolution fusion | flops 34389098496 | bytes 58720256 | tf_op jit(solution)/shard_map/dot_general | solution.py:20
  224.2 43.0 %convolution_convert_fusion = bf16[4096,4096]{1,0:T(8,128)(2,1)} fusion(bf16[4096,1024]{1,0:T(8,128)(2,1)} %fusion.4, bf16[4096,1024]{1,0:T(8,128)(2,1)} %param.8), kind=kOutput, calls=%fused_computation | convolution fusion | flops 34376515584 | bytes 50331648 | tf_op jit(solution)/shard_map/dot_general | solution.py:22
  267.2 0.0 reduce-scatter.2.cloned.1.call-update
  267.2 82.6 %all-gather.5.cloned.1.call-done = bf16[4096,4096]{1,0:T(8,128)(2,1)} async-done(((bf16[256,4096]{1,0:T(8,128)(2,1)}), bf16[4096,4096]{1,0:T(8,128)(2,1)}) %all-gather.5.cloned.1.call-update) | async-done | bytes 33554448 | tf_op jit(solution)/shard_map/all_gather | solution.py:18
  349.8 43.2 %convert_bitcast_fusion = bf16[4096,1024]{0,1:T(8,128)(2,1)} fusion(bf16[4096,1024]{1,0:T(8,128)(2,1)} %fusion.4, bf16[4096,4096]{1,0:T(8,128)(2,1)} %all-gather.5.cloned.1.call-done), kind=kOutput, calls=%fused_computation.10 | convolution fusion | flops 34363932672 | bytes 50331648 | tf_op jit(solution)/shard_map/dot_general | solution.py:12
  393.0 11.9 %copy.8 = bf16[4096,1024]{1,0:T(8,128)(2,1)} copy(bf16[4096,1024]{0,1:T(8,128)(2,1)} %convert_bitcast_fusion) | data formatting | bytes 16777216
  404.9 43.1 %fusion.9 = bf16[1024,4096]{1,0:T(8,128)(2,1)} fusion(bf16[4096,4096]{1,0:T(8,128)(2,1)} %all-gather.3.cloned.1.call-done, bf16[4096,1024]{1,0:T(8,128)(2,1)} %param.7), kind=kOutput, calls=%fused_computation.12 | convolution fusion | flops 34380709888 | bytes 50331648 | tf_op jit(solution)/shard_map/dot_general | solution.py:12
  448.0 234.8 %reduce-scatter.2.cloned.1.call-done = bf16[256,4096]{1,0:T(8,128)(2,1)} async-done(((bf16[4096,4096]{1,0:T(8,128)(2,1)}), bf16[256,4096]{1,0:T(8,128)(2,1)}) %reduce-scatter.2.cloned.1.call-update) | async-done | bytes 2097168 | tf_op jit(solution)/shard_map/reduce_scatter | solution.py:23
Async XLA Ops:
  7.2 173.1 %all-gather.3.cloned.1.call-start = ((), (), s32[]{:S(2)}) async-start(), calls=%async_computation.1 | async-start | bytes 35651584 | tf_op jit(solution)/shard_map/all_gather | solution.py:17
  7.9 341.9 %all-gather.5.cloned.1.call-start = ((), (), s32[]{:S(2)}) async-start(), calls=%async_computation.3 | async-start | bytes 35651584 | tf_op jit(solution)/shard_map/all_gather | solution.py:18
  8.6 674.2 %reduce-scatter.2.cloned.1.call-start = ((), (), s32[]{:S(2)}) async-start(), calls=%async_computation.2 | async-start | bytes 35651584 | tf_op jit(solution)/shard_map/reduce_scatter | solution.py:23
Sparse Core Ops, SparseCore 0:
  9.6 170.6 all-gather.2
  181.9 167.9 all-gather.4
  354.7 328.1 reduce-scatter.1

commit v2 on v1

v2 whole, which is shorter than its diff:
```python
import functools

import jax
import jax.numpy as jnp
from jax import lax
from jax.experimental import pallas as pl
from jax.experimental.pallas import tpu as pltpu
from jax.sharding import PartitionSpec as P

MESH = pl.DeviceIdType.MESH
F32, BF16 = jnp.float32, jnp.bfloat16

X1, XA, XB, XY, L, A, B = range(7)
END = [(L, 0), (B, 0), (B, 1), (L, 1), (X1, 0), (XA, 0), (B, 2), (B, 3), (L, 2), (A, 0), (L, 3), (XB, 0), (XA, 1), (A, 1),
       (XB, 1), (B, 4), (B, 5), (A, 2), (XA, 2), (XB, 2), (XB, 3), (XB, 4), (XB, 5), (XY, 0), (XY, 1), (B, 7), (XY, 2),
       (A, 3), (XY, 3), (B, 6)]
MID = [(L, 0), (L, 1), (XA, 0), (XA, 1), (XB, 0), (XB, 2), (B, 0), (B, 1), (L, 2), (X1, 0), (XB, 1), (XA, 2), (L, 3),
       (XB, 3), (A, 0), (B, 2), (B, 3), (XB, 4), (A, 1), (XB, 5), (B, 4), (B, 5), (A, 2), (XY, 0), (XY, 1), (B, 7), (XY, 2),
       (A, 3), (XY, 3), (B, 6)]


def act(pre):
    return jnp.square(jax.nn.relu(pre))


def over_tokens(a, b):
    return lax.dot_general(a, b, (((0,), (0,)), ((), ())), preferred_element_type=F32)


def kernel(ca, x_ref, d_pre, w_o, w_p, dx_ref, x_all, r_l, r_a, r_b, r_f,
           wo, wp, dpo, dpp, total, got, s_a, s_b,
           load_sem, got_sem, own_sem, pair_sem, xr, xp, xs, lr, ar, br, fr, as_, bs):
    rows, cols = x_ref.shape
    cb = cols - ca
    tile = min(256, ca, cb)
    dp, tp = lax.axis_index("dp"), lax.axis_index("tp")
    c, z, y = lax.rem(tp, 2), lax.rem(tp // 2, 4), tp // 8
    mid = jnp.logical_or(z == 1, z == 2)
    low, high = z > 0, z < 3

    def device(y, z, c):
        return (dp, (y * 4 + z) * 2 + c)

    across, other = device(1 - y, z, c), device(y, z, 1 - c)
    up, down = device(y, jnp.minimum(z + 1, 3), c), device(y, jnp.maximum(z - 1, 0), c)

    def put(src, dst, send, recv, to):
        return pltpu.make_async_remote_copy(src, dst, send, recv, device_id=to, device_id_type=MESH)

    def arrive(dst, recv):
        put(dst, dst, recv, recv, other).wait_recv()

    def part(block, p):
        return block.at[:, pl.ds(ca * p, (ca, cb)[p])]

    def x_part(p, ys, zs, cs):
        return part(x_all.at[(ys * 4 + zs) * 2 + cs], p)

    def x_put(route, p, ys, zs, src=None):
        to = (up, down, across, other)[route]
        here = x_part(p, ys, zs, c)
        recv = (xp if route == 3 else xr).at[p, ys, zs]
        return put(here if src is None else src, here, xs.at[p, ys, zs, route], recv, to)

    def dest(i):
        flip = z + 1 - 2 * lax.rem(z, 2)
        return jnp.where(i == 3, z, jnp.where(i == 2, flip, jnp.where(z < 2, 3 - i, i)))

    def x_line(p, ys, zs, do):
        @pl.when(jnp.logical_and(mid, zs < z))
        def _():
            do(x_put(0, p, ys, zs))

        @pl.when(jnp.logical_and(mid, zs > z))
        def _():
            do(x_put(1, p, ys, zs))

    def x_both(p, ys, do, src=None):
        @pl.when(high)
        def _():
            do(x_put(0, p, ys, z, src))

        @pl.when(low)
        def _():
            do(x_put(1, p, ys, z, src))

    def x_own(do):
        for p in (0, 1):
            src = part(x_ref, p)
            do(x_put(2, p, y, z, src))
            x_both(p, y, do, src)
        for p in (0, 1):
            do(x_put(3, p, y, z, part(x_ref, p)))

    def x_event(kind, a, do, first):
        def on(p, ys, zs):
            if first:
                arrive(x_part(p, ys, zs, c), xr.at[p, ys, zs])
            do(x_put(3, p, ys, zs))

        if kind == X1:
            on(1, 1 - y, z)
            x_both(1, 1 - y, do)
        elif kind == XA:
            zs = dest(2 - a)
            on(0, y, zs)
            x_line(0, y, zs, do)
            do(x_put(2, 0, y, zs))
        elif kind == XB:
            zs, ys = dest(2 - a // 2), lax.rem(y + lax.rem(a, 2), 2)
            on(1, ys, zs)
            x_line(1, ys, zs, do)
        else:
            on(0, 1 - y, dest(3 - a))

    def start(copy):
        copy.start()

    def done(copy):
        copy.wait_send()

    def term(ys, zs, p):
        d = ys * 4 + zs

        @pl.loop(0, (ca, cb)[p] // tile)
        def _(n):
            from_ = pl.ds(pl.multiple_of(n * tile + ca * p, tile), tile)
            to = pl.ds(pl.multiple_of(n * tile, tile), tile)
            total[:, to] = (jnp.dot(dpo[d], wo[:, from_], preferred_element_type=F32)
                            + jnp.dot(dpp[d], wp[:, from_], preferred_element_type=F32))

    def absorb(src, recv, p):
        n = (ca, cb)[p]
        arrive(src, recv)
        copy = pltpu.make_async_copy(src, got.at[:, pl.ds(0, n)], got_sem)
        copy.start()
        copy.wait()

        @pl.loop(0, n // tile)
        def _(k):
            at = pl.ds(pl.multiple_of(k * tile, tile), tile)
            total[:, at] += got[:, at].astype(F32)

    def store(dst, p, offset=0):
        @pl.loop(0, (ca, cb)[p] // tile)
        def _(k):
            at = pl.ds(pl.multiple_of(k * tile, tile), tile)
            dst[:, pl.ds(pl.multiple_of(k * tile + offset, tile), tile)] = total[:, at].astype(BF16)

    def across_put(i):
        return put(s_a.at[i], r_l.at[dest(i)], as_.at[i], lr.at[dest(i)], across)

    def a_put(i, to):
        side = jnp.where(dest(i) > z, 0, 1)
        return put(s_a.at[4 + i], r_a.at[side, dest(i)], as_.at[4 + i], ar.at[side, dest(i)], to)

    def b_put(i, o, to):
        side, ys = jnp.where(dest(i) > z, 0, 1), lax.rem(y + o, 2)
        return put(s_b.at[i * 2 + o], r_b.at[side, ys, dest(i)], bs.at[i * 2 + o], br.at[side, ys, dest(i)], to)

    def along(i, make, do):
        @pl.when(jnp.logical_and(i < 3, dest(i) > z))
        def _():
            do(make(up))

        @pl.when(jnp.logical_and(i < 3, dest(i) < z))
        def _():
            do(make(down))

    def final_put():
        return put(s_b.at[6], r_f, bs.at[6], fr, across)

    def sides(i, slot, sem, p):
        d = dest(i)

        @pl.when(jnp.logical_or(jnp.logical_and(i == 3, low), jnp.logical_and(mid, d > z)))
        def _():
            absorb(slot(0, d), sem(0, d), p)

        @pl.when(jnp.logical_or(jnp.logical_and(i == 3, high), jnp.logical_and(mid, d < z)))
        def _():
            absorb(slot(1, d), sem(1, d), p)

    def event_l(i):
        term(1 - y, dest(i), 0)
        store(s_a.at[i], 0)
        across_put(i).start()

    def event_a(i):
        term(y, dest(i), 0)
        absorb(r_l.at[dest(i)], lr.at[dest(i)], 0)
        sides(i, lambda s, d: r_a.at[s, d], lambda s, d: ar.at[s, d], 0)

        @pl.when(i < 3)
        def _():
            store(s_a.at[4 + i], 0)

        along(i, functools.partial(a_put, i), start)

        @pl.when(i == 3)
        def _():
            store(dx_ref, 0)

    def event_b(a):
        i, o = a // 2, lax.rem(a, 2)
        ys = lax.rem(y + o, 2)
        term(ys, dest(i), 1)
        sides(i, lambda s, d: r_b.at[s, ys, d], lambda s, d: br.at[s, ys, d], 1)

        @pl.when(a == 6)
        def _():
            absorb(r_f, fr, 1)
            store(dx_ref, 1, ca)

        @pl.when(a != 6)
        def _():
            store(s_b.at[jnp.minimum(a, 6)], 1)

        along(i, functools.partial(b_put, i, o), start)

        @pl.when(a == 7)
        def _():
            final_put().start()

    barrier = pltpu.get_barrier_semaphore()
    for peer in (across, other):
        pl.semaphore_signal(barrier, inc=1, device_id=peer, device_id_type=MESH)

    @pl.when(high)
    def _():
        pl.semaphore_signal(barrier, inc=1, device_id=up, device_id_type=MESH)

    @pl.when(low)
    def _():
        pl.semaphore_signal(barrier, inc=1, device_id=down, device_id_type=MESH)

    pl.semaphore_wait(barrier, jnp.where(mid, 4, 3))

    pair = put(d_pre.at[:, 1 - c], dpp, pair_sem.at[0], pair_sem.at[1], other)
    pair.start()
    loads = [pltpu.make_async_copy(src, dst, load_sem.at[k])
             for k, (src, dst) in enumerate(((d_pre.at[:, c], dpo), (w_o, wo), (w_p, wp)))]
    for copy in loads:
        copy.start()
    x_own(start)
    own = pltpu.make_async_copy(x_ref, x_all.at[tp], own_sem)
    own.start()
    for copy in loads:
        copy.wait()
    pair.wait()

    @pl.loop(0, len(END))
    def _(e):
        code = sum(jnp.where(e == k, jnp.where(mid, m[0] * 8 + m[1], n[0] * 8 + n[1]), 0)
                   for k, (m, n) in enumerate(zip(MID, END)))
        kind, a = code // 8, lax.rem(code, 8)
        for k in (X1, XA, XB, XY):
            pl.when(kind == k)(functools.partial(x_event, k, a, start, True))
        pl.when(kind == L)(functools.partial(event_l, a))
        pl.when(kind == A)(functools.partial(event_a, a))
        pl.when(kind == B)(functools.partial(event_b, a))

    own.wait()
    for p in (0, 1):
        @pl.loop(0, 8)
        def _(s, p=p):
            arrive(x_part(p, s // 4, lax.rem(s, 4), 1 - c), xp.at[p, s // 4, lax.rem(s, 4)])
    x_own(done)
    x_event(X1, 0, done, False)
    for k, n in ((XA, 3), (XB, 6), (XY, 4)):
        @pl.loop(0, n)
        def _(a, k=k):
            x_event(k, a, done, False)

    @pl.loop(0, 4)
    def _(i):
        across_put(i).wait_send()

    @pl.loop(0, 3)
    def _(i):
        along(i, functools.partial(a_put, i), done)
        for o in (0, 1):
            along(i, functools.partial(b_put, i, o), done)

    final_put().wait_send()


def exchange(x, d_pre, w_o, w_p, ca):
    rows, cols = x.shape
    depth = d_pre.shape[-1]
    cb = cols - ca
    any_, vmem = pl.BlockSpec(memory_space=pl.ANY), pl.BlockSpec(memory_space=pltpu.VMEM)
    dma = pltpu.SemaphoreType.DMA
    outs = [(rows, cols), (16, rows, cols), (4, rows, ca), (2, 4, rows, ca), (2, 2, 4, rows, cb), (rows, cb)]
    dx, x_all, *_ = pl.pallas_call(
        functools.partial(kernel, ca),
        out_shape=[jax.ShapeDtypeStruct(s, BF16) for s in outs],
        in_specs=[vmem, any_, any_, any_],
        out_specs=[vmem] + [any_] * 5,
        scratch_shapes=[
            pltpu.VMEM((depth, cols), BF16), pltpu.VMEM((depth, cols), BF16),
            pltpu.VMEM((8, rows, depth), BF16), pltpu.VMEM((8, rows, depth), BF16),
            pltpu.VMEM((rows, ca), F32), pltpu.VMEM((rows, ca), BF16),
            pltpu.VMEM((7, rows, ca), BF16), pltpu.VMEM((7, rows, cb), BF16),
            dma((3,)), dma, dma, dma((2,)), dma((2, 2, 4)), dma((2, 2, 4)), dma((2, 2, 4, 4)),
            dma((4,)), dma((2, 4)), dma((2, 2, 4)), dma, dma((7,)), dma((7,)),
        ],
        compiler_params=pltpu.CompilerParams(
            collective_id=0, has_side_effects=True, vmem_limit_bytes=60 * 2**20),
    )(x, d_pre.reshape(8, 2, rows, depth), w_o, w_p)
    return dx, x_all.reshape(16 * rows, cols)


def solution(mesh, ca=2560):
    def step(x, dy, pre, w_in, w_down):
        w_o = w_in.T
        w_p = lax.ppermute(w_o, "tp", [(i, i ^ 1) for i in range(16)])
        dy = lax.all_gather(dy, "tp", tiled=True)
        hidden, back = jax.vjp(act, pre.astype(F32))
        d_hidden = jnp.dot(dy, w_down.T, preferred_element_type=F32)
        d_pre = back(d_hidden)[0].astype(BF16)
        dw_down = over_tokens(hidden.astype(BF16), dy).astype(BF16)
        dx, x = exchange(x, d_pre, w_o, w_p, ca)
        dw_in = over_tokens(x, d_pre).astype(BF16)
        return dx, dw_in, dw_down

    rows = P(("dp", "tp"), None)
    return jax.shard_map(
        step,
        mesh=mesh,
        in_specs=(rows, rows, P("dp", "tp"), P(None, "tp"), P("tp", None)),
        out_specs=(rows, P("dp", "tp"), rows),
        check_vma=False,
    )
```

time: 690 us -> 603 us (0.87)
  waiting for transfers between devices: 490 us -> 161 us
  Pallas kernels: 0 us -> 283 us
  matrix products: 173 us -> 130 us
    pallas_call x0 -> x1, Pallas kernels: none -> 283 us  [exchange(): pl.pallas_call(functools.partial(kernel, ca), out_shape=[jax.ShapeDtypeSt...]
    reduce_scatter x1 -> x0, waiting for transfers between devices: 235 us -> none  [step(): dx = lax.psum_scatter(dx, 'tp', scatter_dimension=0, tiled=True)]
    all_gather x1 -> x0, waiting for transfers between devices: 82.6 us -> none  [step(): x = lax.all_gather(x, 'tp', tiled=True)]
    dot_general x4 -> x3, matrix products: 173 us -> 130 us  [the longest x2 86.5 us: over_tokens(): lax.dot_general(a, b, (((0,), (0,)), ((), ())), preferred_element_type=F32)]
    all_gather x1, waiting for transfers between devices: 172 us -> 160 us  [step(): dy = lax.all_gather(dy, 'tp', tiled=True)]
  transfers between devices with their start and end apart: 3 -> 2, of which waited for: 3 -> 1; matrix products, arithmetic and copies ran while one was open for 27% -> 9% of each run, Pallas kernels for 0% -> 0%
where the time goes in v2:
time: 603 us; the launch traced here: 602 us
  Pallas kernels  283 us (47%)
  waiting for transfers between devices  161 us (27%)
  matrix products  130 us (22%)
  between operations  14 us (2%)
  local copies, waits for them, and re-layouts  13.2 us (2%)
    pallas_call x1, Pallas kernels, exchange(): pl.pallas_call(functools.partial(kernel, ca), out_shape=[jax.ShapeDtypeSt...  283 us
    all_gather x1, waiting for transfers between devices, step(): dy = lax.all_gather(dy, 'tp', tiled=True)  160 us
    dot_general x2, matrix products, over_tokens(): lax.dot_general(a, b, (((0,), (0,)), ((), ())), preferred_element_type=F32)  86.5 us
    dot_general x1, matrix products, step(): d_hidden = jnp.dot(dy, w_down.T, preferred_element_type=F32)  43.9 us
    unnamed x4, local copies, waits for them, and re-layouts  13.2 us
  transfers between devices with their start and end apart: 2, of which 1 were waited for; matrix products, arithmetic and copies ran while one was open for 9% of the time, Pallas kernels for 0%

profile of v2, /device:TPU:0, one launch (start us, length us, event | category | flops | bytes accessed | tf_op | source)
XLA Modules:
  0.0 601.9 jit_solution(14193437380586340028)
XLA Ops:
  7.2 0.0 all-gather.2.cloned.1.call-start
  7.2 0.7 all-gather.2.cloned.1.call-update
  7.9 11.9 %copy.8 = bf16[4096,1024]{0,1:T(8,128)(2,1)} copy(bf16[4096,1024]{1,0:T(8,128)(2,1)} %param.8) | data formatting | bytes 16777216 | tf_op args[3]
  19.8 0.5 collective-permute-start
  20.3 160.0 %all-gather.2.cloned.1.call-done = bf16[4096,4096]{1,0:T(8,128)(2,1)} async-done(((bf16[256,4096]{1,0:T(8,128)(2,1)}), bf16[4096,4096]{1,0:T(8,128)(2,1)}) %all-gather.2.cloned.1.call-update) | async-done | bytes 33554448 | tf_op jit(solution)/shard_map/all_gather | solution.py:318
  180.3 43.9 %fusion.4 = bf16[4096,1024]{1,0:T(8,128)(2,1)} fusion(bf16[4096,1024]{1,0:T(8,128)(2,1)} %param.7, bf16[4096,4096]{1,0:T(8,128)(2,1)} %all-gather.2.cloned.1.call-done, bf16[1024,4096]{1,0:T(8,128)(2,1)} %param.9), kind=kOutput, calls=%fused_computation.6 | convolution fusion | flops 34389098496 | bytes 58720256 | tf_op jit(solution)/shard_map/dot_general | solution.py:320
  224.2 0.0 collective-permute-done.w_p
  224.2 283.1 %shard_map.76 = (bf16[256,4096]{1,0:T(8,128)(2,1)}, bf16[16,256,4096]{2,1,0:T(8,128)(2,1)}, bf16[4,256,2560]{2,1,0:T(8,128)(2,1)}, bf16[2,4,256,2560]{3,2,1,0:T(...) custom-call(bf16[256,4096]{1,0:T(8,128)(2,1)} %x_ref.1, ...), custom_call_target="tpu_custom_call" | custom-call | tf_op jit(solution)/shard_map/pallas_call | solution.py:295
  507.3 43.2 %convolution_convert_fusion = bf16[4096,1024]{1,0:T(8,128)(2,1)} fusion(bf16[4096,4096]{1,0:T(8,128)(2,1)} %bitcast.11, bf16[4096,1024]{1,0:T(8,128)(2,1)} %fusion.4), kind=kOutput, calls=%fused_computation.11 | convolution fusion | flops 34363932672 | bytes 50331648 | tf_op jit(solution)/shard_map/dot_general | solution.py:27
  550.5 0.0 copy-start
  550.5 43.2 %fusion.9 = bf16[1024,4096]{1,0:T(8,128)(2,1)} fusion(bf16[4096,4096]{1,0:T(8,128)(2,1)} %all-gather.2.cloned.1.call-done, bf16[4096,1024]{1,0:T(8,128)(2,1)} %param.7), kind=kOutput, calls=%fused_computation.10 | convolution fusion | flops 34380709888 | bytes 50331648 | tf_op jit(solution)/shard_map/dot_general | solution.py:27
  593.8 0.0 copy-done
  593.8 1.3 copy.10
Async XLA Ops:
  7.2 173.1 %all-gather.2.cloned.1.call-start = ((), (), s32[]{:S(2)}) async-start(), calls=%async_computation | async-start | bytes 35651584 | tf_op jit(solution)/shard_map/all_gather | solution.py:318
  19.8 204.4 %collective-permute-start = (bf16[1024,4096]{1,0:T(8,128)(2,1)}, bf16[1024,4096]{1,0:T(8,128)(2,1)}, u32[]{:S(2)}, u32[]{:S(2)}) collective-permute-start(bf16[1024,4096]{1,0:T(8,128)(2,1)} %bitcast.8), channel_id=1, source_target_pairs={{0,1},{1,0},{2,3},{3,2},{4,5},{5,4},{6,7},{7,6},{8,9},{9,8},{10,11... | collective-permute-start | bytes 25165832 | tf_op jit(solution)/shard_map/ppermute | solution.py:317
  550.5 43.3 %copy-start = (bf16[256,4096]{1,0:T(8,128)(2,1)S(1)}, bf16[256,4096]{1,0:T(8,128)(2,1)}, u32[]{:S(2)}) copy-start(bf16[256,4096]{1,0:T(8,128)(2,1)} %get-tuple-element.10) | copy-start | bytes 6291460
Sparse Core Ops, SparseCore 0:
  9.6 170.6 all-gather.1

commit v3 on v1

v3 whole, which is shorter than its diff:
```python
import functools

import jax
import jax.numpy as jnp
from jax import lax
from jax.experimental import pallas as pl
from jax.experimental.pallas import tpu as pltpu
from jax.sharding import PartitionSpec as P

MESH = pl.DeviceIdType.MESH
F32, BF16 = jnp.float32, jnp.bfloat16

G0, G1, GA, GB, GY, D, W, L, A, B, DD, DI, DJ = range(13)
CG, CA = 3072, 1536
END = [
    (G1, 0), (GY, 0), (G0, 8), (D, 4), (GA, 1), (GA, 0), (GB, 2), (D, 2), (G1, 8), (W, 2), (B, 2), (GB, 0), (D, 1), (GY,
    2), (D, 0), (GB, 4), (GA, 2), (W, 4), (L, 3), (D, 3), (W, 3), (B, 0), (GB, 3), (GB, 5), (GB, 1), (D, 6), (GY, 1),
    (W, 6), (L, 1), (B, 3), (GY, 3), (D, 5), (D, 7), (W, 7), (B, 1), (GA, 8), (W, 5), (B, 5), (W, 1), (B, 4), (GY, 8),
    (L, 0), (GA, 9), (A, 1), (DD, 1), (DD, 3), (L, 2), (GY, 9), (DD, 2), (DD, 0), (GB, 11), (GB, 8), (GB, 10), (GY, 10),
    (GB, 9), (GA, 10), (A, 0), (GB, 13), (DI, 0), (DI, 1), (DI, 3), (A, 2), (GB, 12), (DI, 2), (GY, 11), (B, 7), (DJ,
    0), (DJ, 3), (DJ, 2), (DJ, 1), (W, 0), (A, 3), (B, 6),
]
MID = [
    (D, 0), (GA, 0), (GA, 1), (GB, 0), (GB, 1), (GY, 0), (GB, 2), (G1, 0), (D, 2), (GA, 2), (D, 4), (GA, 8), (GB, 4),
    (D, 3), (GB, 5), (D, 1), (GY, 1), (GB, 3), (GY, 2), (D, 5), (GY, 3), (G0, 8), (W, 5), (L, 2), (D, 7), (D, 6), (DD,
    0), (GA, 9), (GB, 8), (W, 4), (L, 3), (W, 7), (L, 0), (W, 3), (B, 0), (DD, 1), (GB, 9), (DD, 2), (G1, 8), (W, 6),
    (L, 1), (GA, 10), (B, 3), (DD, 3), (B, 1), (GY, 8), (GB, 10), (GB, 11), (W, 2), (B, 2), (GB, 13), (GB, 12), (GY,
    10), (GY, 9), (B, 7), (DI, 0), (DI, 2), (B, 5), (DI, 1), (A, 1), (W, 1), (B, 4), (A, 0), (GY, 11), (DI, 3), (DJ, 0),
    (A, 2), (DJ, 2), (DJ, 1), (W, 0), (A, 3), (DJ, 3), (B, 6),
]


def kernel(cg, ca, dy, x, pre, w_in, w_down, dx, dw_in, dw_down, all_, d_all, part_in, r_l, r_a, r_b, r_f, s_a, s_b,
           wo, wp, wd, dpo, dpp, dps, rows_v, pre_v, total, got, stage, acc, ost,
           load_sem, got_sem, own_sem, pair_sem, dp_sem, d_sem, o_sem, gr, gp, gs, lr, ar, br, fr, as_, bs):
    rows, cols = dy.shape
    depth = w_down.shape[0]
    cuts = (cg, cols - cg)
    widths = (ca, cols - ca)
    tile = min(256, ca, cols - ca)
    ff = min(256, depth)
    wide = ost.shape[0]
    dp, tp = lax.axis_index("dp"), lax.axis_index("tp")
    c, z, y = lax.rem(tp, 2), lax.rem(tp // 2, 4), tp // 8
    mid = jnp.logical_or(z == 1, z == 2)
    low, high = z > 0, z < 3

    def device(y, z, c):
        return (dp, (y * 4 + z) * 2 + c)

    across, other = device(1 - y, z, c), device(y, z, 1 - c)
    up, down = device(y, jnp.minimum(z + 1, 3), c), device(y, jnp.maximum(z - 1, 0), c)

    def put(src, dst, send, recv, to):
        return pltpu.make_async_remote_copy(src, dst, send, recv, device_id=to, device_id_type=MESH)

    def arrive(dst, recv):
        put(dst, dst, recv, recv, other).wait_recv()

    def start(copy):
        copy.start()

    def done(copy):
        copy.wait_send()

    def dest(i):
        flip = z + 1 - 2 * lax.rem(z, 2)
        return jnp.where(i == 3, z, jnp.where(i == 2, flip, jnp.where(z < 2, 3 - i, i)))

    def cut(block, p):
        return block.at[:, pl.ds(cg * p, cuts[p])]

    def g_part(g, p, ys, zs, cs):
        return cut(all_.at[g, (ys * 4 + zs) * 2 + cs], p)

    def g_put(route, g, p, ys, zs, src=None):
        to = (up, down, across, other)[route]
        here = g_part(g, p, ys, zs, c)
        recv = (gp if route == 3 else gr).at[g, p, ys, zs]
        return put(here if src is None else src, here, gs.at[g, p, ys, zs, route], recv, to)

    def g_line(g, p, ys, zs, do):
        @pl.when(jnp.logical_and(mid, zs < z))
        def _():
            do(g_put(0, g, p, ys, zs))

        @pl.when(jnp.logical_and(mid, zs > z))
        def _():
            do(g_put(1, g, p, ys, zs))

    def g_both(g, p, ys, do, src=None):
        @pl.when(high)
        def _():
            do(g_put(0, g, p, ys, z, src))

        @pl.when(low)
        def _():
            do(g_put(1, g, p, ys, z, src))

    def g_own(g, do):
        block = (dy, x)[g]
        for p in (0, 1):
            src = cut(block, p)
            do(g_put(2, g, p, y, z, src))
            g_both(g, p, y, do, src)
        for p in (0, 1):
            do(g_put(3, g, p, y, z, cut(block, p)))

    def g_event(kind, g, a, do, first):
        def on(p, ys, zs):
            if first:
                arrive(g_part(g, p, ys, zs, c), gr.at[g, p, ys, zs])
            do(g_put(3, g, p, ys, zs))

        if kind == G1:
            on(1, 1 - y, z)
            g_both(g, 1, 1 - y, do)
        elif kind == GA:
            zs = dest(2 - a)
            on(0, y, zs)
            g_line(g, 0, y, zs, do)
            do(g_put(2, g, 0, y, zs))
        elif kind == GB:
            zs, ys = dest(2 - a // 2), lax.rem(y + lax.rem(a, 2), 2)
            on(1, ys, zs)
            g_line(g, 1, ys, zs, do)
        else:
            on(0, 1 - y, dest(3 - a))

    def from_other(g, s):
        for p in (0, 1):
            arrive(g_part(g, p, s // 4, lax.rem(s, 4), 1 - c), gp.at[g, p, s // 4, lax.rem(s, 4)])

    def make_d_pre(a):
        s = lax.rem(y + a // 4, 2) * 4 + dest(3 - lax.rem(a, 4))
        from_other(0, s)
        ids = (s * 2 + 1 - c, s * 2 + c)
        loads = []
        for k, b in enumerate(ids):
            for n, (src, dst) in enumerate(((all_.at[0, b], rows_v.at[k]), (pre.at[b], pre_v.at[k]))):
                loads.append(pltpu.make_async_copy(src, dst, load_sem.at[k * 2 + n]))
        for copy in loads:
            copy.start()
        copies = []
        for k, (b, out) in enumerate(zip(ids, (dps, dpo.at[s]))):
            loads[2 * k].wait()
            loads[2 * k + 1].wait()

            @pl.loop(0, depth // ff)
            def _(n, k=k, out=out):
                at = pl.ds(pl.multiple_of(n * ff, ff), ff)
                back = lax.dot_general(rows_v[k], wd[at, :], (((1,), (1,)), ((), ())), preferred_element_type=F32)
                kept = pre_v[k, :, at].astype(F32)
                out[:, at] = jnp.where(kept > 0, back * (2 * kept), 0).astype(BF16)

            if k == 0:
                copies.append(put(dps, dpp.at[s], d_sem.at[0], dp_sem.at[s], other))
            copies.append(pltpu.make_async_copy(out, d_all.at[b], d_sem.at[1 + k]))
            for copy in copies[-2 + k:]:
                copy.start()
        copies[0].wait_send()
        copies[1].wait()
        copies[2].wait()

    def wait_d_pre(a):
        s = lax.rem(y + a // 4, 2) * 4 + dest(3 - lax.rem(a, 4))
        arrive(dpp.at[s], dp_sem.at[s])

    def term(ys, zs, p):
        d = ys * 4 + zs
        dims = (((1,), (1,)), ((), ()))

        @pl.loop(0, widths[p] // tile)
        def _(n):
            from_ = pl.ds(pl.multiple_of(n * tile + ca * p, tile), tile)
            to = pl.ds(pl.multiple_of(n * tile, tile), tile)
            total[:, to] = (lax.dot_general(dpo[d], wo[from_, :], dims, preferred_element_type=F32)
                            + lax.dot_general(dpp[d], wp[from_, :], dims, preferred_element_type=F32))

    def absorb(src, recv, p):
        n = widths[p]
        arrive(src, recv)
        copy = pltpu.make_async_copy(src, got.at[:, pl.ds(0, n)], got_sem)
        copy.start()
        copy.wait()

        @pl.loop(0, n // tile)
        def _(k):
            at = pl.ds(pl.multiple_of(k * tile, tile), tile)
            total[:, at] += got[:, at].astype(F32)

    def store(dst, p):
        @pl.loop(0, widths[p] // tile)
        def _(k):
            at = pl.ds(pl.multiple_of(k * tile, tile), tile)
            stage[:, at] = total[:, at].astype(BF16)

        copy = pltpu.make_async_copy(stage.at[:, pl.ds(0, widths[p])], dst, got_sem)
        copy.start()
        copy.wait()

    def across_put(i):
        return put(s_a.at[i], r_l.at[dest(i)], as_.at[i], lr.at[dest(i)], across)

    def a_put(i, to):
        side = jnp.where(dest(i) > z, 0, 1)
        return put(s_a.at[4 + i], r_a.at[side, dest(i)], as_.at[4 + i], ar.at[side, dest(i)], to)

    def b_put(i, o, to):
        side, ys = jnp.where(dest(i) > z, 0, 1), lax.rem(y + o, 2)
        return put(s_b.at[i * 2 + o], r_b.at[side, ys, dest(i)], bs.at[i * 2 + o], br.at[side, ys, dest(i)], to)

    def along(i, make, do):
        @pl.when(jnp.logical_and(i < 3, dest(i) > z))
        def _():
            do(make(up))

        @pl.when(jnp.logical_and(i < 3, dest(i) < z))
        def _():
            do(make(down))

    def final_put():
        return put(s_b.at[6], r_f, bs.at[6], fr, across)

    def sides(i, slot, sem, p):
        d = dest(i)

        @pl.when(jnp.logical_or(jnp.logical_and(i == 3, low), jnp.logical_and(mid, d > z)))
        def _():
            absorb(slot(0, d), sem(0, d), p)

        @pl.when(jnp.logical_or(jnp.logical_and(i == 3, high), jnp.logical_and(mid, d < z)))
        def _():
            absorb(slot(1, d), sem(1, d), p)

    def event_l(i):
        term(1 - y, dest(i), 0)
        store(s_a.at[i], 0)
        across_put(i).start()

    def event_a(i):
        term(y, dest(i), 0)
        absorb(r_l.at[dest(i)], lr.at[dest(i)], 0)
        sides(i, lambda s, d: r_a.at[s, d], lambda s, d: ar.at[s, d], 0)

        @pl.when(i < 3)
        def _():
            store(s_a.at[4 + i], 0)

        along(i, functools.partial(a_put, i), start)

        @pl.when(i == 3)
        def _():
            store(dx.at[:, pl.ds(0, ca)], 0)

    def event_b(a):
        i, o = a // 2, lax.rem(a, 2)
        ys = lax.rem(y + o, 2)
        term(ys, dest(i), 1)
        sides(i, lambda s, d: r_b.at[s, ys, d], lambda s, d: br.at[s, ys, d], 1)

        @pl.when(a == 6)
        def _():
            absorb(r_f, fr, 1)
            store(dx.at[:, pl.ds(ca, cols - ca)], 1)

        @pl.when(a != 6)
        def _():
            store(s_b.at[jnp.where(a == 7, 6, jnp.minimum(a, 5))], 1)

        along(i, functools.partial(b_put, i, o), start)

        @pl.when(a == 7)
        def _():
            final_put().start()

    over = (((0,), (0,)), ((), ()))

    def near(k):
        return lax.rem(y + lax.rem(k, 2), 2) * 4 + dest(3 - k // 2)

    def event_dd(t):
        acc[...] = jnp.zeros_like(acc)

        def add(kept, rows_):
            hidden = jnp.square(jnp.maximum(kept[...].astype(F32), 0)).astype(BF16)
            hidden = hidden.reshape(2 * rows, depth)
            acc[...] += lax.dot_general(hidden, rows_[0].reshape(2 * rows, wide), over, preferred_element_type=F32)

        pltpu.emit_pipeline(
            add, grid=(8,),
            in_specs=[pl.BlockSpec((2, rows, depth), lambda k: (k, 0, 0)),
                      pl.BlockSpec((1, 2, rows, wide), lambda k: (0, k, 0, t))],
        )(pre, all_)
        ost[...] = acc[...].astype(BF16)
        copy = pltpu.make_async_copy(ost, dw_down.at[:, pl.ds(pl.multiple_of(t * wide, wide), wide)], o_sem)
        copy.start()
        copy.wait()

    def x_tile(t, k0, n):
        def add(rows_, d):
            acc[...] += lax.dot_general(rows_[0].reshape(2 * rows, wide), d[...].reshape(2 * rows, depth), over,
                                        preferred_element_type=F32)

        pltpu.emit_pipeline(
            add, grid=(n,),
            in_specs=[pl.BlockSpec((1, 2, rows, wide), lambda k: (1, near(k0 + k), 0, t)),
                      pl.BlockSpec((2, rows, depth), lambda k: (near(k0 + k), 0, 0))],
        )(all_, d_all)

    def event_di(t):
        @pl.when(t == 0)
        def _():
            @pl.loop(0, 6)
            def _(k):
                from_other(1, near(k))

        acc[...] = jnp.zeros_like(acc)
        x_tile(t, 0, 6)
        copy = pltpu.make_async_copy(acc, part_in.at[t], o_sem)
        copy.start()
        copy.wait()

    def event_dj(t):
        @pl.when(t == 0)
        def _():
            @pl.loop(6, 8)
            def _(k):
                from_other(1, near(k))

        copy = pltpu.make_async_copy(part_in.at[t], acc, o_sem)
        copy.start()
        copy.wait()
        x_tile(t, 6, 2)
        ost[...] = acc[...].astype(BF16)
        copy = pltpu.make_async_copy(ost, dw_in.at[pl.ds(pl.multiple_of(t * wide, wide), wide), :], o_sem)
        copy.start()
        copy.wait()

    barrier = pltpu.get_barrier_semaphore()
    for peer in (across, other):
        pl.semaphore_signal(barrier, inc=1, device_id=peer, device_id_type=MESH)

    @pl.when(high)
    def _():
        pl.semaphore_signal(barrier, inc=1, device_id=up, device_id_type=MESH)

    @pl.when(low)
    def _():
        pl.semaphore_signal(barrier, inc=1, device_id=down, device_id_type=MESH)

    pl.semaphore_wait(barrier, jnp.where(mid, 4, 3))

    g_own(0, start)
    into = [pltpu.make_async_copy(src, rows_v.at[g], own_sem.at[g]) for g, src in enumerate((dy, x))]
    loads = [pltpu.make_async_copy(src, dst, load_sem.at[k]) for k, (src, dst) in enumerate(((w_down, wd), (w_in, wo)))]
    for copy in into + loads:
        copy.start()
    pair = put(w_in, wp, pair_sem.at[0], pair_sem.at[1], other)
    pair.start()
    own = [pltpu.make_async_copy(rows_v.at[g], all_.at[g, tp], own_sem.at[g]) for g in (0, 1)]
    for a, b in zip(into, own):
        a.wait()
        b.start()
    for copy in loads + own:
        copy.wait()
    pair.wait()

    @pl.loop(0, len(END))
    def _(e):
        code = sum(jnp.where(e == k, jnp.where(mid, m[0] * 16 + m[1], n[0] * 16 + n[1]), 0)
                   for k, (m, n) in enumerate(zip(MID, END)))
        kind, a = code // 16, lax.rem(code, 16)
        g, b = a // 8, lax.rem(a, 8)
        pl.when(kind == G0)(functools.partial(g_own, 1, start))
        for k in (G1, GA, GB, GY):
            pl.when(kind == k)(functools.partial(g_event, k, g, b, start, True))
        for k, do in ((D, make_d_pre), (W, wait_d_pre), (L, event_l), (A, event_a), (B, event_b),
                      (DD, event_dd), (DI, event_di), (DJ, event_dj)):
            pl.when(kind == k)(functools.partial(do, a))

    g_own(0, done)
    g_own(1, done)

    @pl.loop(0, 2)
    def _(g):
        g_event(G1, g, 0, done, False)
        for k, n in ((GA, 3), (GB, 6), (GY, 4)):
            @pl.loop(0, n)
            def _(a, k=k):
                g_event(k, g, a, done, False)

    @pl.loop(0, 4)
    def _(i):
        across_put(i).wait_send()

    @pl.loop(0, 3)
    def _(i):
        along(i, functools.partial(a_put, i), done)
        for o in (0, 1):
            along(i, functools.partial(b_put, i, o), done)

    final_put().wait_send()


def solution(mesh, cg=CG, ca=CA):
    def step(x, dy, pre, w_in, w_down):
        rows, cols = x.shape
        depth = w_down.shape[0]
        cb = cols - ca
        wide = cols // 4
        dma, vmem = pltpu.SemaphoreType.DMA, pltpu.VMEM
        outs = [(rows, cols), (cols, depth), (depth, cols), (2, 16, rows, cols), (16, rows, depth), (4, wide, depth),
                (4, rows, ca), (2, 4, rows, ca), (2, 2, 4, rows, cb), (rows, cb), (7, rows, ca), (7, rows, cb)]
        any_ = pl.BlockSpec(memory_space=pl.ANY)
        widest = max(ca, cb)
        out = pl.pallas_call(
            functools.partial(kernel, cg, ca),
            out_shape=[jax.ShapeDtypeStruct(s, F32 if k == 5 else BF16) for k, s in enumerate(outs)],
            in_specs=[any_] * 5,
            out_specs=[any_] * len(outs),
            scratch_shapes=[
                vmem((cols, depth), BF16), vmem((cols, depth), BF16), vmem((depth, cols), BF16),
                vmem((8, rows, depth), BF16), vmem((8, rows, depth), BF16), vmem((rows, depth), BF16),
                vmem((2, rows, cols), BF16), vmem((2, rows, depth), BF16),
                vmem((rows, widest), F32), vmem((rows, widest), BF16), vmem((rows, widest), BF16),
                vmem((wide, wide), F32), vmem((wide, wide), BF16),
                dma((4,)), dma, dma((2,)), dma((2,)), dma((8,)), dma((3,)), dma,
                dma((2, 2, 2, 4)), dma((2, 2, 2, 4)), dma((2, 2, 2, 4, 4)),
                dma((4,)), dma((2, 4)), dma((2, 2, 4)), dma, dma((7,)), dma((7,)),
            ],
            compiler_params=pltpu.CompilerParams(
                collective_id=0, has_side_effects=True, vmem_limit_bytes=62 * 2**20),
        )(dy, x, pre.reshape(16, rows, depth), w_in, w_down)
        return out[:3]

    rows = P(("dp", "tp"), None)
    return jax.shard_map(
        step,
        mesh=mesh,
        in_specs=(rows, rows, P("dp", "tp"), P(None, "tp"), P("tp", None)),
        out_specs=(rows, P("dp", "tp"), rows),
        check_vma=False,
    )
```

time: 690 us -> 466 us (0.68)
  waiting for transfers between devices: 490 us -> 0 us
  Pallas kernels: 0 us -> 444 us
  matrix products: 173 us -> 0 us
  between operations: 13.7 us -> 0.64 us
  local copies, waits for them, and re-layouts: 11.9 us -> 18.8 us
    pallas_call x0 -> x1, Pallas kernels: none -> 444 us  [step(): pl.pallas_call(functools.partial(kernel, cg, ca), out_shape=[jax.ShapeDty...]
    all_gather x2 -> x0, waiting for transfers between devices: 254 us -> none  [the longest x1 172 us: step(): dy = lax.all_gather(dy, 'tp', tiled=True)]
    reduce_scatter x1 -> x0, waiting for transfers between devices: 235 us -> none  [step(): dx = lax.psum_scatter(dx, 'tp', scatter_dimension=0, tiled=True)]
    dot_general x4 -> x0, matrix products: 173 us -> none  [the longest x2 86.3 us: over_tokens(): lax.dot_general(a, b, (((0,), (0,)), ((), ())), preferred_element_type=jn...]
    unnamed x1 -> x3, local copies, waits for them, and re-layouts: 11.9 us -> 18.8 us
  transfers between devices with their start and end apart: 3 -> 0, of which waited for: 3 -> 0; matrix products, arithmetic and copies ran while one was open for 27% -> 0% of each run, Pallas kernels for 0% -> 0%
where the time goes in v3:
time: 466 us; the launch traced here: 464 us
  Pallas kernels  444 us (95%)
  local copies, waits for them, and re-layouts  18.8 us (4%)
    pallas_call x1, Pallas kernels, step(): pl.pallas_call(functools.partial(kernel, cg, ca), out_shape=[jax.ShapeDty...  444 us
    unnamed x3, local copies, waits for them, and re-layouts  18.8 us

profile of v3, /device:TPU:0, one launch (start us, length us, event | category | flops | bytes accessed | tf_op | source)
XLA Modules:
  0.0 463.5 jit_solution(5138860719303788209)
XLA Ops:
  0.6 444.1 %shard_map.76 = (bf16[256,4096]{1,0:T(8,128)(2,1)}, bf16[4096,1024]{1,0:T(8,128)(2,1)}, bf16[1024,4096]{1,0:T(8,128)(2,1)}, bf16[2,16,256,4096]{3,2,1,0:T(8,128)...) custom-call(bf16[256,4096]{1,0:T(8,128)(2,1)} %dy.1, ...), custom_call_target="tpu_custom_call" | custom-call | tf_op jit(solution)/shard_map/pallas_call | solution.py:417
  444.8 3.1 copy.11
  447.9 7.8 %copy.12 = bf16[4096,1024]{1,0:T(8,128)(2,1)} copy(bf16[4096,1024]{1,0:T(8,128)(2,1)} %get-tuple-element.13) | data formatting | bytes 16777216
  455.7 7.9 %copy.13 = bf16[1024,4096]{1,0:T(8,128)(2,1)} copy(bf16[1024,4096]{1,0:T(8,128)(2,1)} %get-tuple-element.14) | data formatting | bytes 16777216

commit v4 on v3

--- a/solution.py
+++ b/solution.py
@@ -11,22 +11,22 @@
 F32, BF16 = jnp.float32, jnp.bfloat16
 
 G0, G1, GA, GB, GY, D, W, L, A, B, DD, DI, DJ = range(13)
-CG, CA = 3072, 1536
+CG, CA = 3328, 1024
 END = [
-    (G1, 0), (GY, 0), (G0, 8), (D, 4), (GA, 1), (GA, 0), (GB, 2), (D, 2), (G1, 8), (W, 2), (B, 2), (GB, 0), (D, 1), (GY,
-    2), (D, 0), (GB, 4), (GA, 2), (W, 4), (L, 3), (D, 3), (W, 3), (B, 0), (GB, 3), (GB, 5), (GB, 1), (D, 6), (GY, 1),
-    (W, 6), (L, 1), (B, 3), (GY, 3), (D, 5), (D, 7), (W, 7), (B, 1), (GA, 8), (W, 5), (B, 5), (W, 1), (B, 4), (GY, 8),
-    (L, 0), (GA, 9), (A, 1), (DD, 1), (DD, 3), (L, 2), (GY, 9), (DD, 2), (DD, 0), (GB, 11), (GB, 8), (GB, 10), (GY, 10),
-    (GB, 9), (GA, 10), (A, 0), (GB, 13), (DI, 0), (DI, 1), (DI, 3), (A, 2), (GB, 12), (DI, 2), (GY, 11), (B, 7), (DJ,
-    0), (DJ, 3), (DJ, 2), (DJ, 1), (W, 0), (A, 3), (B, 6),
+    (GY, 0), (G1, 0), (G0, 8), (D, 4), (GA, 1), (D, 0), (GB, 2), (G1, 8), (GB, 0), (D, 2), (W, 2), (B, 2), (GA, 2), (GA,
+    0), (GB, 4), (D, 1), (D, 3), (GY, 2), (GB, 3), (W, 3), (B, 0), (D, 6), (GB, 5), (GY, 8), (GY, 3), (W, 6), (L, 1),
+    (D, 7), (W, 7), (B, 1), (B, 3), (W, 1), (B, 4), (GB, 1), (GY, 1), (GA, 8), (A, 1), (D, 5), (DD, 3), (GB, 8), (L, 0),
+    (GA, 9), (DD, 1), (DD, 0), (DD, 2), (W, 5), (L, 2), (GB, 9), (A, 0), (GA, 10), (GB, 10), (B, 5), (GY, 10), (GY, 9),
+    (GB, 11), (W, 4), (L, 3), (DI, 0), (DI, 3), (GB, 13), (DI, 1), (B, 7), (GY, 11), (A, 2), (GB, 12), (DI, 2), (DJ, 0),
+    (DJ, 2), (DJ, 3), (DJ, 1), (W, 0), (B, 6), (A, 3),
 ]
 MID = [
-    (D, 0), (GA, 0), (GA, 1), (GB, 0), (GB, 1), (GY, 0), (GB, 2), (G1, 0), (D, 2), (GA, 2), (D, 4), (GA, 8), (GB, 4),
-    (D, 3), (GB, 5), (D, 1), (GY, 1), (GB, 3), (GY, 2), (D, 5), (GY, 3), (G0, 8), (W, 5), (L, 2), (D, 7), (D, 6), (DD,
-    0), (GA, 9), (GB, 8), (W, 4), (L, 3), (W, 7), (L, 0), (W, 3), (B, 0), (DD, 1), (GB, 9), (DD, 2), (G1, 8), (W, 6),
-    (L, 1), (GA, 10), (B, 3), (DD, 3), (B, 1), (GY, 8), (GB, 10), (GB, 11), (W, 2), (B, 2), (GB, 13), (GB, 12), (GY,
-    10), (GY, 9), (B, 7), (DI, 0), (DI, 2), (B, 5), (DI, 1), (A, 1), (W, 1), (B, 4), (A, 0), (GY, 11), (DI, 3), (DJ, 0),
-    (A, 2), (DJ, 2), (DJ, 1), (W, 0), (A, 3), (DJ, 3), (B, 6),
+    (GA, 0), (GY, 0), (GA, 1), (GB, 0), (D, 0), (GB, 1), (GB, 2), (D, 2), (D, 1), (GA, 2), (GB, 4), (G1, 0), (D, 4),
+    (GB, 3), (GB, 5), (G0, 8), (D, 3), (GY, 1), (GA, 8), (GY, 2), (D, 6), (D, 5), (GA, 9), (W, 2), (B, 2), (GY, 3), (D,
+    7), (DD, 1), (GB, 9), (GB, 10), (DD, 0), (DD, 3), (G1, 8), (DD, 2), (W, 7), (B, 1), (GY, 9), (GA, 10), (W, 4), (L,
+    3), (GB, 8), (W, 5), (L, 2), (W, 6), (L, 1), (L, 0), (GY, 8), (GB, 11), (W, 3), (B, 0), (GB, 13), (B, 3), (GY, 10),
+    (B, 5), (DI, 0), (DI, 2), (DI, 1), (GB, 12), (GY, 11), (DI, 3), (W, 1), (B, 4), (DJ, 0), (DJ, 3), (A, 1), (B, 7),
+    (A, 0), (DJ, 2), (DJ, 1), (A, 2), (W, 0), (A, 3), (B, 6),
 ]
 
 
@@ -401,6 +401,23 @@
             along(i, functools.partial(b_put, i, o), done)
 
     final_put().wait_send()
+
+
+def carry(dx, dw_in, dw_down, dx_out, dw_in_out, dw_down_out, flat, tall, sems):
+    pieces = [(dx, dx_out, flat.at[0])]
+    for k in range(4):
+        for src, dst, buf in ((dw_in, dw_in_out, tall), (dw_down, dw_down_out, flat.at[pl.ds(1, 4)])):
+            at = pl.ds(k * buf.shape[1], buf.shape[1])
+            pieces.append((src.at[at], dst.at[at], buf.at[k]))
+    ins = [pltpu.make_async_copy(src, buf, sems.at[0, k]) for k, (src, _, buf) in enumerate(pieces)]
+    outs = [pltpu.make_async_copy(buf, dst, sems.at[1, k]) for k, (_, dst, buf) in enumerate(pieces)]
+    for copy in ins:
+        copy.start()
+    for a, b in zip(ins, outs):
+        a.wait()
+        b.start()
+    for copy in outs:
+        copy.wait()
 
 
 def solution(mesh, cg=CG, ca=CA):
@@ -432,7 +449,15 @@
             compiler_params=pltpu.CompilerParams(
                 collective_id=0, has_side_effects=True, vmem_limit_bytes=62 * 2**20),
         )(dy, x, pre.reshape(16, rows, depth), w_in, w_down)
-        return out[:3]
+        return pl.pallas_call(
+            carry,
+            out_shape=[jax.ShapeDtypeStruct(s, BF16) for s in outs[:3]],
+            in_specs=[any_] * 3,
+            out_specs=[any_] * 3,
+            scratch_shapes=[vmem((5, depth // 4, cols), BF16), vmem((4, wide, depth), BF16), dma((2, 9))],
+            compiler_params=pltpu.CompilerParams(vmem_limit_bytes=62 * 2**20),
+            cost_estimate=pl.CostEstimate(flops=0, bytes_accessed=36 * 2**20, transcendentals=0),
+        )(*out[:3])
 
     rows = P(("dp", "tp"), None)
     return jax.shard_map(

time: 466 us -> 442 us (0.948)
  local copies, waits for them, and re-layouts: 18.8 us -> 0 us
  Pallas kernels: 444 us -> 438 us
    pallas_call x1, Pallas kernels: 444 us -> 425 us  [step(): pl.pallas_call(functools.partial(kernel, cg, ca), out_shape=[jax.ShapeDty...]
    unnamed x3 -> x0, local copies, waits for them, and re-layouts: 18.8 us -> none
    pallas_call x0 -> x1, Pallas kernels: none -> 12.9 us  [step(): pl.pallas_call(carry, out_shape=[jax.ShapeDtypeStruct(s, BF16) for s in o...]
where the time goes in v4:
time: 442 us; the launch traced here: 438 us
  Pallas kernels  438 us (99%)
    pallas_call x1, Pallas kernels, step(): pl.pallas_call(functools.partial(kernel, cg, ca), out_shape=[jax.ShapeDty...  425 us
    pallas_call x1, Pallas kernels, step(): pl.pallas_call(carry, out_shape=[jax.ShapeDtypeStruct(s, BF16) for s in o...  12.9 us

profile of v4, /device:TPU:0, one launch (start us, length us, event | category | flops | bytes accessed | tf_op | source)
XLA Modules:
  0.0 438.4 jit_solution(11906949814573093869)
XLA Ops:
  0.6 424.9 %shard_map.76 = (bf16[256,4096]{1,0:T(8,128)(2,1)}, bf16[4096,1024]{1,0:T(8,128)(2,1)}, bf16[1024,4096]{1,0:T(8,128)(2,1)}, bf16[2,16,256,4096]{3,2,1,0:T(8,128)...) custom-call(bf16[256,4096]{1,0:T(8,128)(2,1)} %dy.1, ...), custom_call_target="tpu_custom_call" | custom-call | tf_op jit(solution)/shard_map/pallas_call | solution.py:434
  425.5 12.9 %shard_map.77 = (bf16[256,4096]{1,0:T(8,128)(2,1)}, bf16[4096,1024]{1,0:T(8,128)(2,1)}, bf16[1024,4096]{1,0:T(8,128)(2,1)}) custom-call(bf16[256,4096]{1,0:T(8,128)(2,1)} %get-tuple-element.6.dx, bf16[4096,1024]{1,0:T(8,128)(2,1)} %get-tuple-element.7.dw_in, bf16[1024,4096]{1,0:T(8,128)(2,1)} %get-tuple-element.8.dw_down), custom_call_target="tpu_custom_call" | custom-call | bytes 37748736 | tf_op jit(solution)/shard_map/pallas_call | solution.py:452

commit v5 on v4

--- a/solution.py
+++ b/solution.py
@@ -16,21 +16,21 @@
     (GY, 0), (G1, 0), (G0, 8), (D, 4), (GA, 1), (D, 0), (GB, 2), (G1, 8), (GB, 0), (D, 2), (W, 2), (B, 2), (GA, 2), (GA,
     0), (GB, 4), (D, 1), (D, 3), (GY, 2), (GB, 3), (W, 3), (B, 0), (D, 6), (GB, 5), (GY, 8), (GY, 3), (W, 6), (L, 1),
     (D, 7), (W, 7), (B, 1), (B, 3), (W, 1), (B, 4), (GB, 1), (GY, 1), (GA, 8), (A, 1), (D, 5), (DD, 3), (GB, 8), (L, 0),
-    (GA, 9), (DD, 1), (DD, 0), (DD, 2), (W, 5), (L, 2), (GB, 9), (A, 0), (GA, 10), (GB, 10), (B, 5), (GY, 10), (GY, 9),
-    (GB, 11), (W, 4), (L, 3), (DI, 0), (DI, 3), (GB, 13), (DI, 1), (B, 7), (GY, 11), (A, 2), (GB, 12), (DI, 2), (DJ, 0),
-    (DJ, 2), (DJ, 3), (DJ, 1), (W, 0), (B, 6), (A, 3),
+    (GA, 9), (DD, 1), (DD, 0), (DD, 2), (W, 5), (L, 2), (GB, 9), (A, 0), (W, 0), (A, 3), (B, 6), (GA, 10), (GB, 10), (B,
+    5), (GY, 10), (GY, 9), (GB, 11), (W, 4), (L, 3), (DI, 0), (DI, 3), (GB, 13), (DI, 1), (B, 7), (GY, 11), (A, 2), (GB,
+    12), (DI, 2), (DJ, 0), (DJ, 2), (DJ, 3), (DJ, 1),
 ]
 MID = [
     (GA, 0), (GY, 0), (GA, 1), (GB, 0), (D, 0), (GB, 1), (GB, 2), (D, 2), (D, 1), (GA, 2), (GB, 4), (G1, 0), (D, 4),
     (GB, 3), (GB, 5), (G0, 8), (D, 3), (GY, 1), (GA, 8), (GY, 2), (D, 6), (D, 5), (GA, 9), (W, 2), (B, 2), (GY, 3), (D,
     7), (DD, 1), (GB, 9), (GB, 10), (DD, 0), (DD, 3), (G1, 8), (DD, 2), (W, 7), (B, 1), (GY, 9), (GA, 10), (W, 4), (L,
-    3), (GB, 8), (W, 5), (L, 2), (W, 6), (L, 1), (L, 0), (GY, 8), (GB, 11), (W, 3), (B, 0), (GB, 13), (B, 3), (GY, 10),
-    (B, 5), (DI, 0), (DI, 2), (DI, 1), (GB, 12), (GY, 11), (DI, 3), (W, 1), (B, 4), (DJ, 0), (DJ, 3), (A, 1), (B, 7),
-    (A, 0), (DJ, 2), (DJ, 1), (A, 2), (W, 0), (A, 3), (B, 6),
+    3), (GB, 8), (W, 5), (L, 2), (W, 6), (L, 1), (L, 0), (GY, 8), (GB, 11), (W, 3), (B, 0), (GB, 13), (B, 3), (W, 0),
+    (A, 3), (B, 6), (GY, 10), (B, 5), (DI, 0), (DI, 2), (DI, 1), (GB, 12), (GY, 11), (DI, 3), (W, 1), (B, 4), (DJ, 0),
+    (DJ, 3), (A, 1), (B, 7), (A, 0), (DJ, 2), (DJ, 1), (A, 2),
 ]
 
 
-def kernel(cg, ca, dy, x, pre, w_in, w_down, dx, dw_in, dw_down, all_, d_all, part_in, r_l, r_a, r_b, r_f, s_a, s_b,
+def kernel(cg, ca, dy, x, pre, w_in, w_down, own_term, dw_in, dw_down, all_, d_all, part_in, r_l, r_a, r_b, r_f, s_a, s_b,
            wo, wp, wd, dpo, dpp, dps, rows_v, pre_v, total, got, stage, acc, ost,
            load_sem, got_sem, own_sem, pair_sem, dp_sem, d_sem, o_sem, gr, gp, gs, lr, ar, br, fr, as_, bs):
     rows, cols = dy.shape
@@ -199,6 +199,11 @@
         copy.start()
         copy.wait()
 
+    def keep(p):
+        copy = pltpu.make_async_copy(total.at[:, pl.ds(0, widths[p])], own_term.at[:, pl.ds(ca * p, widths[p])], got_sem)
+        copy.start()
+        copy.wait()
+
     def across_put(i):
         return put(s_a.at[i], r_l.at[dest(i)], as_.at[i], lr.at[dest(i)], across)
 
@@ -240,32 +245,31 @@
 
     def event_a(i):
         term(y, dest(i), 0)
-        absorb(r_l.at[dest(i)], lr.at[dest(i)], 0)
-        sides(i, lambda s, d: r_a.at[s, d], lambda s, d: ar.at[s, d], 0)
 
         @pl.when(i < 3)
         def _():
+            absorb(r_l.at[dest(i)], lr.at[dest(i)], 0)
+            sides(i, lambda s, d: r_a.at[s, d], lambda s, d: ar.at[s, d], 0)
             store(s_a.at[4 + i], 0)
 
         along(i, functools.partial(a_put, i), start)
 
         @pl.when(i == 3)
         def _():
-            store(dx.at[:, pl.ds(0, ca)], 0)
+            keep(0)
 
     def event_b(a):
         i, o = a // 2, lax.rem(a, 2)
         ys = lax.rem(y + o, 2)
         term(ys, dest(i), 1)
-        sides(i, lambda s, d: r_b.at[s, ys, d], lambda s, d: br.at[s, ys, d], 1)
 
         @pl.when(a == 6)
         def _():
-            absorb(r_f, fr, 1)
-            store(dx.at[:, pl.ds(ca, cols - ca)], 1)
+            keep(1)
 
         @pl.when(a != 6)
         def _():
+            sides(i, lambda s, d: r_b.at[s, ys, d], lambda s, d: br.at[s, ys, d], 1)
             store(s_b.at[jnp.where(a == 7, 6, jnp.minimum(a, 5))], 1)
 
         along(i, functools.partial(b_put, i, o), start)
@@ -379,6 +383,14 @@
                       (DD, event_dd), (DI, event_di), (DJ, event_dj)):
             pl.when(kind == k)(functools.partial(do, a))
 
+    arrive(r_l.at[z], lr.at[z])
+    arrive(r_f, fr)
+    for side, there in ((0, low), (1, high)):
+        @pl.when(there)
+        def _(side=side):
+            arrive(r_a.at[side, z], ar.at[side, z])
+            arrive(r_b.at[side, y, z], br.at[side, y, z])
+
     g_own(0, done)
     g_own(1, done)
 
@@ -403,10 +415,23 @@
     final_put().wait_send()
 
 
-def carry(dx, dw_in, dw_down, dx_out, dw_in_out, dw_down_out, flat, tall, sems):
-    pieces = [(dx, dx_out, flat.at[0])]
+def finish(ca, own_term, dw_in, dw_down, r_l, r_a, r_b, r_f, dx_out, dw_in_out, dw_down_out,
+           total, part_a, part_b, dx, flat, tall, sems, sum_sems):
+    cols = total.shape[1]
+    tp = lax.axis_index("tp")
+    z, y = lax.rem(tp // 2, 4), tp // 8
+    low, high, always = z > 0, z < 3, z >= 0
+    sums = [(always, own_term, total)]
+    sums += [(there, src, part_a.at[k]) for k, (there, src) in enumerate(
+        ((always, r_l.at[z]), (low, r_a.at[0, z]), (high, r_a.at[1, z])))]
+    sums += [(there, src, part_b.at[k]) for k, (there, src) in enumerate(
+        ((low, r_b.at[0, y, z]), (high, r_b.at[1, y, z]), (always, r_f)))]
+    sums = [(there, pltpu.make_async_copy(src, dst, sum_sems.at[k]), dst) for k, (there, src, dst) in enumerate(sums)]
+    for there, copy, _ in sums:
+        pl.when(there)(copy.start)
+    pieces = []
     for k in range(4):
-        for src, dst, buf in ((dw_in, dw_in_out, tall), (dw_down, dw_down_out, flat.at[pl.ds(1, 4)])):
+        for src, dst, buf in ((dw_in, dw_in_out, tall), (dw_down, dw_down_out, flat)):
             at = pl.ds(k * buf.shape[1], buf.shape[1])
             pieces.append((src.at[at], dst.at[at], buf.at[k]))
     ins = [pltpu.make_async_copy(src, buf, sems.at[0, k]) for k, (src, _, buf) in enumerate(pieces)]
@@ -416,7 +441,18 @@
     for a, b in zip(ins, outs):
         a.wait()
         b.start()
-    for copy in outs:
+    for k, (there, copy, buf) in enumerate(sums):
+        @pl.when(there)
+        def _(k=k, copy=copy, buf=buf):
+            copy.wait()
+            if k:
+                at = pl.ds(0, ca) if k < 4 else pl.ds(ca, cols - ca)
+                total[:, at] += buf[...].astype(F32)
+
+    dx[...] = total[...].astype(BF16)
+    out = pltpu.make_async_copy(dx, dx_out, sum_sems.at[0])
+    out.start()
+    for copy in outs + [out]:
         copy.wait()
 
 
@@ -433,7 +469,7 @@
         widest = max(ca, cb)
         out = pl.pallas_call(
             functools.partial(kernel, cg, ca),
-            out_shape=[jax.ShapeDtypeStruct(s, F32 if k == 5 else BF16) for k, s in enumerate(outs)],
+            out_shape=[jax.ShapeDtypeStruct(s, F32 if k in (0, 5) else BF16) for k, s in enumerate(outs)],
             in_specs=[any_] * 5,
             out_specs=[any_] * len(outs),
             scratch_shapes=[
@@ -449,15 +485,18 @@
             compiler_params=pltpu.CompilerParams(
                 collective_id=0, has_side_effects=True, vmem_limit_bytes=62 * 2**20),
         )(dy, x, pre.reshape(16, rows, depth), w_in, w_down)
+        results = [(rows, cols), (cols, depth), (depth, cols)]
         return pl.pallas_call(
-            carry,
-            out_shape=[jax.ShapeDtypeStruct(s, BF16) for s in outs[:3]],
-            in_specs=[any_] * 3,
+            functools.partial(finish, ca),
+            out_shape=[jax.ShapeDtypeStruct(s, BF16) for s in results],
+            in_specs=[any_] * 7,
             out_specs=[any_] * 3,
-            scratch_shapes=[vmem((5, depth // 4, cols), BF16), vmem((4, wide, depth), BF16), dma((2, 9))],
+            scratch_shapes=[
+                vmem((rows, cols), F32), vmem((3, rows, ca), BF16), vmem((3, rows, cb), BF16), vmem((rows, cols), BF16),
+                vmem((4, depth // 4, cols), BF16), vmem((4, wide, depth), BF16), dma((2, 8)), dma((7,))],
             compiler_params=pltpu.CompilerParams(vmem_limit_bytes=62 * 2**20),
-            cost_estimate=pl.CostEstimate(flops=0, bytes_accessed=36 * 2**20, transcendentals=0),
-        )(*out[:3])
+            cost_estimate=pl.CostEstimate(flops=0, bytes_accessed=44 * 2**20, transcendentals=0),
+        )(*out[:3], *out[6:10])
 
     rows = P(("dp", "tp"), None)
     return jax.shard_map(

time: 442 us -> 439 us (level)
  no operation moved by 1% of the time
where the time goes in v5:
time: 439 us; the launch traced here: 438 us
  Pallas kernels  437 us (100%)
    pallas_call x1, Pallas kernels, step(): pl.pallas_call(functools.partial(kernel, cg, ca), out_shape=[jax.ShapeDty...  422 us
    pallas_call x1, Pallas kernels, step(): pl.pallas_call(functools.partial(finish, ca), out_shape=[jax.ShapeDtypeSt...  15.2 us

profile of v5, /device:TPU:0, one launch (start us, length us, event | category | flops | bytes accessed | tf_op | source)
XLA Modules:
  0.0 437.7 jit_solution(4135635990009874523)
XLA Ops:
  0.6 421.8 %shard_map.76 = (f32[256,4096]{1,0:T(8,128)}, bf16[4096,1024]{1,0:T(8,128)(2,1)}, bf16[1024,4096]{1,0:T(8,128)(2,1)}, bf16[2,16,256,4096]{3,2,1,0:T(8,128)(2,1)}...) custom-call(bf16[256,4096]{1,0:T(8,128)(2,1)} %dy.1, ...), custom_call_target="tpu_custom_call" | custom-call | tf_op jit(solution)/shard_map/pallas_call | solution.py:470
  422.5 15.2 %shard_map.77 = (bf16[256,4096]{1,0:T(8,128)(2,1)}, bf16[4096,1024]{1,0:T(8,128)(2,1)}, bf16[1024,4096]{1,0:T(8,128)(2,1)}) custom-call(f32[256,4096]{1,0:T(8,128)} %get-tuple-element.10.own_term, bf16[4096,1024]{1,0:T(8,128)(2,1)} %get-tuple-element.11.dw_in, bf16[1024,4096]{1,0:T(8,128)(2,1)} %get-tuple-element.12.dw_down, ...), custom_call_target="tpu_custom_call" | custom-call | bytes 46137344 | tf_op jit(solution)/shard_map/pallas_call | solution.py:489
